TPU v7x, 32 devices: a 4x2x2 block of a 4x4x8 slice. The times are simulated.
32 devices in a mesh: dp: 4 (over y, z), tp: 8 (over x, core).
Axes of the slice: x: 4, y: 2, z: 2, core: 2. Of those that a mesh axis runs over, the one named last changes fastest.
The devices are a block of a 4x4x8 slice.
Arguments:
- hidden: bfloat16 [8, 3840], P('dp'), parts along dimension 0
- positions: int32 [8], P('dp'), parts along dimension 0
- k_local: bfloat16 [8, 1024, 8, 256], P('dp', None, 'tp'), parts along dimension 0
- v_local: bfloat16 [8, 1024, 8, 256], P('dp', None, 'tp'), parts along dimension 0
- k_global: bfloat16 [8, 4096, 8, 256], P('dp', None, 'tp'), parts along dimension 0
- v_global: bfloat16 [8, 4096, 8, 256], P('dp', None, 'tp'), parts along dimension 0
- w_query: bfloat16 [2, 3840, 4096], P(None, None, 'tp')
- w_key: bfloat16 [2, 3840, 2048], P(None, None, 'tp')
- w_value: bfloat16 [2, 3840, 2048], P(None, None, 'tp')
- w_out: bfloat16 [2, 4096, 3840], P(None, 'tp')
- w_gate: bfloat16 [2, 3840, 15360], P(None, None, 'tp')
- w_up: bfloat16 [2, 3840, 15360], P(None, None, 'tp')
- w_down: bfloat16 [2, 15360, 3840], P(None, 'tp')
- norm_scale: float32 [2, 4, 3840], replicated
Outputs:
- output 1: bfloat16 [8, 3840], P('dp'), parts along dimension 0
- output 2: bfloat16 [8, 1024, 8, 256], P('dp', None, 'tp'), parts along dimension 0
- output 3: bfloat16 [8, 1024, 8, 256], P('dp', None, 'tp'), parts along dimension 0
- output 4: bfloat16 [8, 4096, 8, 256], P('dp', None, 'tp'), parts along dimension 0
- output 5: bfloat16 [8, 4096, 8, 256], P('dp', None, 'tp'), parts along dimension 0
There are 4 independent parts. A program takes and returns all parts, laid end to end along the dimension named above; an argument that names none is the same for every part.
All inputs are finite; a program needn't handle non-finite values.
Results may differ from a plain program's by a relative error of at most 0.02.
Values are sent between devices in bfloat16 or wider.
A program may use at most 768 MiB of HBM per device.

v0:
```python
import jax
import jax.numpy as jnp
from jax import lax
from jax.sharding import PartitionSpec as P

SOFT_CAP = 50.0
NORM_EPS = 1e-6
ROPE_BASE = 10000.0
NEG_FILL = -1e30


def rms_norm(values, gain_row):
    values_f32 = values.astype(jnp.float32)
    inv_rms = lax.rsqrt(jnp.mean(values_f32 * values_f32, axis=-1, keepdims=True) + NORM_EPS)
    return (values_f32 * inv_rms * (1.0 + gain_row)).astype(jnp.bfloat16)


def rotary(projected, positions):
    head_dim = projected.shape[-1]
    half_dim = head_dim // 2
    inv_freq = ROPE_BASE ** (-2.0 * jnp.arange(half_dim, dtype=jnp.float32) / head_dim)
    angles = positions.astype(jnp.float32)[:, None, None] * inv_freq
    cos_part = jnp.cos(angles)
    sin_part = jnp.sin(angles)
    first_half = projected[..., :half_dim]
    second_half = projected[..., half_dim:]
    return jnp.concatenate([first_half * cos_part - second_half * sin_part, second_half * cos_part + first_half * sin_part], axis=-1)


def project_and_store(hidden, positions, k_cache, v_cache, slot_ids, w_query, w_key, w_value, gain_row):
    batch_rows = hidden.shape[0]
    kv_count = k_cache.shape[2]
    head_dim = k_cache.shape[3]
    normed = rms_norm(hidden, gain_row)
    queries = rotary(jnp.dot(normed, w_query, preferred_element_type=jnp.float32).reshape(batch_rows, -1, head_dim), positions)
    key_new = rotary(jnp.dot(normed, w_key, preferred_element_type=jnp.float32).reshape(batch_rows, kv_count, head_dim), positions)
    value_new = jnp.dot(normed, w_value, preferred_element_type=jnp.float32).reshape(batch_rows, kv_count, head_dim)
    slot_iota = lax.broadcasted_iota(jnp.int32, (batch_rows, k_cache.shape[1]), 1)
    slot_hit = (slot_iota == slot_ids[:, None])[:, :, None, None]
    k_cache = jnp.where(slot_hit, key_new.astype(jnp.bfloat16)[:, None], k_cache)
    v_cache = jnp.where(slot_hit, value_new.astype(jnp.bfloat16)[:, None], v_cache)
    grouped = queries.astype(jnp.bfloat16).reshape(batch_rows, kv_count, -1, head_dim)
    return grouped, k_cache, v_cache


def attention(grouped, k_cache, v_cache, key_valid):
    head_dim = grouped.shape[-1]
    logits = jnp.einsum('bgrd,bngd->bgrn', grouped, k_cache, preferred_element_type=jnp.float32) * head_dim ** -0.5
    logits = SOFT_CAP * jnp.tanh(logits / SOFT_CAP)
    if key_valid is not None:
        logits = jnp.where(key_valid[:, None, None, :], logits, NEG_FILL)
    attn_probs = jax.nn.softmax(logits, axis=-1).astype(jnp.bfloat16)
    mixed_heads = jnp.einsum('bgrn,bngd->bgrd', attn_probs, v_cache, preferred_element_type=jnp.float32)
    return mixed_heads.astype(jnp.bfloat16)


def mlp_part(normed, w_gate, w_up, w_down):
    gate_proj = jnp.dot(normed, w_gate, preferred_element_type=jnp.float32)
    up_proj = jnp.dot(normed, w_up, preferred_element_type=jnp.float32)
    hidden_act = (jax.nn.gelu(gate_proj, approximate=True) * up_proj).astype(jnp.bfloat16)
    return jnp.dot(hidden_act, w_down, preferred_element_type=jnp.float32)


def add_normed(hidden, branch_sum, gain_row):
    return (hidden.astype(jnp.float32) + rms_norm(branch_sum, gain_row).astype(jnp.float32)).astype(jnp.bfloat16)


def decoder_layer(hidden, positions, k_cache, v_cache, slot_ids, key_valid, layer_weights, gains):
    w_query, w_key, w_value, w_out, w_gate, w_up, w_down = layer_weights
    grouped, k_cache, v_cache = project_and_store(hidden, positions, k_cache, v_cache, slot_ids, w_query, w_key, w_value, gains[0])
    mixed_heads = attention(grouped, k_cache, v_cache, key_valid)
    attn_part = jnp.dot(mixed_heads.reshape(hidden.shape[0], -1), w_out, preferred_element_type=jnp.float32)
    attn_sum = lax.psum(attn_part.astype(jnp.bfloat16), 'tp')
    hidden = add_normed(hidden, attn_sum, gains[1])
    down_part = mlp_part(rms_norm(hidden, gains[2]), w_gate, w_up, w_down)
    down_sum = lax.psum(down_part.astype(jnp.bfloat16), 'tp')
    hidden = add_normed(hidden, down_sum, gains[3])
    return hidden, k_cache, v_cache


def decode_step(hidden, positions, k_local, v_local, k_global, v_global, w_query, w_key, w_value, w_out, w_gate, w_up, w_down, norm_scale):
    stacks = (w_query, w_key, w_value, w_out, w_gate, w_up, w_down)
    window = k_local.shape[1]
    global_valid = lax.broadcasted_iota(jnp.int32, (hidden.shape[0], k_global.shape[1]), 1) <= positions[:, None]
    hidden, k_local, v_local = decoder_layer(hidden, positions, k_local, v_local, positions % window, None, tuple(stacked[0] for stacked in stacks), norm_scale[0])
    hidden, k_global, v_global = decoder_layer(hidden, positions, k_global, v_global, positions, global_valid, tuple(stacked[1] for stacked in stacks), norm_scale[1])
    return hidden, k_local, v_local, k_global, v_global


def solution(mesh):
    row_spec = P('dp', None)
    cache_spec = P('dp', None, 'tp', None)
    col_split = P(None, None, 'tp')
    row_split = P(None, 'tp', None)
    in_specs = (row_spec, P('dp'), cache_spec, cache_spec, cache_spec, cache_spec, col_split, col_split, col_split, row_split, col_split, col_split, row_split, P())
    out_specs = (row_spec, cache_spec, cache_spec, cache_spec, cache_spec)
    return jax.shard_map(decode_step, mesh=mesh, in_specs=in_specs, out_specs=out_specs, check_vma=False)
```

profile of v0, /device:TPU:81, one launch (start us, length us, event | category | flops | bytes accessed | tf_op | source)
XLA Modules:
  0.0 188.3 jit_solution(13756166139027433606)
XLA Ops:
  0.6 1.5 add_reduce_fusion
  2.2 0.9 fusion.104
  3.0 5.6 %slice_bitcast_fusion = (bf16[512,3840]{0,1:T(8,128)(2,1)}, bf16[512,3840]{0,1:T(8,128)(2,1)}) fusion(bf16[2,3840,512]{2,1,0:T(8,128)(2,1)} %param.20), kind=kLoop, calls=%fused_computation.38 | loop fusion | bytes 15728640 | tf_op jit(solution)/shard_map/dot_general | solution.py:35
  8.7 6.3 %copy.19 = bf16[512,3840]{1,0:T(8,128)(2,1)} copy(bf16[512,3840]{0,1:T(8,128)(2,1)} %get-tuple-element.20) | data formatting | bytes 7864320 | tf_op jit(solution)/shard_map/dot_general | solution.py:35
  15.0 3.4 %fusion.140 = f32[2,2,256]{2,0,1:T(2,128)S(1)} fusion(bf16[2,256,3840]{2,1,0:T(8,128)(2,1)} %bitcast.122, bf16[2,3840]{1,0:T(2,128)(2,1)S(1)} %copy-done.6, f32[2]{0:T(128)S(1)} %add_rsqrt_fusion.7, f32[3840]{0:T(1024)S(1)} %get-tuple-element.11), kind=kOutput, calls=%fused_computation.145 | convolution fusion | flops 7895040 | bytes 3966984 | tf_op jit(solution)/shard_map/dot_general | solution.py:35
  18.3 0.0 copy-done.7
  18.4 0.1 multiply_cosine_fusion.1
  18.5 1.9 %fusion.69 = f32[2,1,256]{2,0,1:T(2,128)S(1)} fusion(bf16[2,3840,256]{2,1,0:T(8,128)(2,1)} %param.21, bf16[2,3840]{1,0:T(2,128)(2,1)S(1)} %copy-done.6, f32[2]{0:T(128)S(1)} %add_rsqrt_fusion.7, f32[3840]{0:T(1024)S(1)} %get-tuple-element.11), kind=kOutput, calls=%fused_computation.64 | convolution fusion | flops 3962880 | bytes 1998856 | tf_op jit(solution)/shard_map/dot_general | solution.py:36
  20.4 0.2 fusion.162
  20.6 0.4 fusion.79
  21.0 0.1 iota_compare_fusion.2
  21.1 0.5 broadcast_select_fusion.3
  21.6 0.0 copy-start.2
  21.6 0.0 copy-start.5
  21.6 0.4 fusion.65
  22.0 0.2 fusion.182
  22.2 0.3 fusion.75
  22.5 2.7 %convolution_convert_fusion.1 = bf16[2,3840]{1,0:T(2,128)(2,1)S(1)} fusion(bf16[2,512]{1,0:T(2,128)(2,1)S(1)} %bitcast.124, bf16[2,512,3840]{2,1,0:T(8,128)(2,1)} %param.23), kind=kOutput, calls=%fused_computation.29 | convolution fusion | flops 7872000 | bytes 3949568 | tf_op jit(solution)/shard_map/dot_general | solution.py:72
  25.3 24.0 %psum.28 = bf16[2,3840]{1,0:T(2,128)(2,1)S(1)} all-reduce(bf16[2,3840]{1,0:T(2,128)(2,1)S(1)} %convolution_convert_fusion.1), channel_id=1, replica_groups=mesh['dp'=4,'tp'=8] {'tp'}, use_global_device_ids=true, to_apply=%region_3.4 | all-reduce | flops 7680 | bytes 30720 | tf_op jit(solution)/shard_map/psum | solution.py:73
  49.3 0.1 fusion.92
  49.4 0.2 fusion.108
  49.6 6.4 %fusion.126 = f32[2,1920]{1,0:T(2,128)S(1)} fusion(bf16[2,3840,1920]{2,1,0:T(8,128)(2,1)} %param.24, bf16[2,3840]{1,0:T(2,128)(2,1)S(1)} %get-tuple-element.18, f32[2]{0:T(128)S(1)} %add_rsqrt_fusion.5, f32[3840]{0:T(1024)S(1)} %get-tuple-element.9), kind=kOutput, calls=%fused_computation.135 | convolution fusion | flops 29552640 | bytes 14791688 | tf_op jit(solution)/shard_map/dot_general | solution.py:58
  56.0 0.0 copy-done.2
  56.0 0.0 copy-done.5
  56.0 11.7 %fusion.25 = bf16[2,3840]{1,0:T(2,128)(2,1)S(1)} fusion(bf16[2,1920,3840]{2,1,0:T(8,128)(2,1)} %param.26, f32[2,1920]{1,0:T(2,128)S(1)} %fusion.126, bf16[2,3840,1920]{2,1,0:T(8,128)(2,1)} %param.25, bf16[2,3840]{1,0:T(2,128)(2,1)S(1)} %get-tuple-element.18, f32[2]{0:T(128)S(1)} %add_rsqrt_fusion.5, f32[3840]{0:T(1024)S(1)} %get-tuple-element.9), kind=kOutput, calls=%fused_computation.26 | convolution fusion | flops 59028480 | bytes 29552648 | tf_op jit(solution)/shard_map/dot_general | solution.py:61
  67.8 23.6 %psum.29 = bf16[2,3840]{1,0:T(2,128)(2,1)S(1)} all-reduce(bf16[2,3840]{1,0:T(2,128)(2,1)S(1)} %fusion.25), channel_id=1, replica_groups=mesh['dp'=4,'tp'=8] {'tp'}, use_global_device_ids=true, to_apply=%region_6.7 | all-reduce | flops 7680 | bytes 30720 | tf_op jit(solution)/shard_map/psum | solution.py:76
  91.4 0.1 fusion.95
  91.5 0.2 fusion.112
  91.8 6.3 %copy.21 = bf16[512,3840]{1,0:T(8,128)(2,1)} copy(bf16[512,3840]{0,1:T(8,128)(2,1)} %get-tuple-element.19) | data formatting | bytes 7864320 | tf_op jit(solution)/shard_map/dot_general | solution.py:35
  98.1 3.4 %fusion.138 = f32[2,2,256]{2,0,1:T(2,128)S(1)} fusion(bf16[2,256,3840]{2,1,0:T(8,128)(2,1)} %bitcast.123, bf16[2,3840]{1,0:T(2,128)(2,1)S(1)} %get-tuple-element.16, f32[2]{0:T(128)S(1)} %add_rsqrt_fusion.3, f32[3840]{0:T(1024)S(1)} %get-tuple-element.7), kind=kOutput, calls=%fused_computation.143 | convolution fusion | flops 7895040 | bytes 3966984 | tf_op jit(solution)/shard_map/dot_general | solution.py:35
  101.5 1.9 %fusion.82 = bf16[2,256]{1,0:T(2,128)(2,1)S(1)} fusion(bf16[2,3840,256]{2,1,0:T(8,128)(2,1)} %param.22, bf16[2,3840]{1,0:T(2,128)(2,1)S(1)} %get-tuple-element.16, f32[2]{0:T(128)S(1)} %add_rsqrt_fusion.3, f32[3840]{0:T(1024)S(1)} %get-tuple-element.7), kind=kOutput, calls=%fused_computation.69 | convolution fusion | flops 3963392 | bytes 1997832 | tf_op jit(solution)/shard_map/dot_general | solution.py:37
  103.4 2.0 %fusion.72 = f32[2,1,256]{2,0,1:T(2,128)S(1)} fusion(bf16[2,3840,256]{2,1,0:T(8,128)(2,1)} %param.21, bf16[2,3840]{1,0:T(2,128)(2,1)S(1)} %get-tuple-element.16, f32[2]{0:T(128)S(1)} %add_rsqrt_fusion.3, f32[3840]{0:T(1024)S(1)} %get-tuple-element.7), kind=kOutput, calls=%fused_computation.65 | convolution fusion | flops 3962880 | bytes 1998856 | tf_op jit(solution)/shard_map/dot_general | solution.py:36
  105.4 0.2 fusion.164
  105.5 0.1 iota_compare_fusion.1
  105.6 6.7 %broadcast_select_fusion.1 = (bf16[2,4096,1,256]{3,1,2,0:T(8,128)(2,1)S(1)}, bf16[2,4096,1,256]{3,1,2,0:T(8,128)(2,1)}) fusion(bf16[2,4096,1,256]{3,1,2,0:T(8,128)(2,1)S(1)} %copy-done.1, pred[2,4096]{1,0:T(4,128)(4,1)S(1)} %get-tuple-element.36, bf16[2,256]{1,0:T(2,128)(2,1)S(1)} %pad_maximum_fusion.3, bf16[2,4096,1,256]{3,1,2,0:T(8,128)(2,1)} %param.19, ...), kind=kLoop, calls=%fused_computation.34 | loop fusion | flops 4194304 | bytes 16787456 | tf_op jit(solution)/shard_map/jit(_where)/select_n | solution.py:40
  112.4 2.0 %copy-done = bf16[2,4096,1,256]{3,1,2,0:T(8,128)(2,1)} copy-done((bf16[2,4096,1,256]{3,1,2,0:T(8,128)(2,1)}, bf16[2,4096,1,256]{3,1,2,0:T(8,128)(2,1)S(1)}, u32[]{:S(2)}) %copy-start) | copy-done | bytes 4194328
  114.4 1.2 fusion.24
  115.6 0.3 fusion.183
  115.9 2.9 %fusion.76 = bf16[1,2,2,256]{3,2,1,0:T(2,128)(2,1)S(1)} fusion(bf16[2,4096,1,256]{3,1,2,0:T(8,128)(2,1)} %get-tuple-element.22, f32[2,2]{1,0:T(2,128)S(1)} %fusion.183, f32[2,2,4096]{2,1,0:T(2,128)S(1)} %fusion.24), kind=kOutput, calls=%fused_computation.67 | convolution fusion | flops 8442883 | bytes 4261904 | tf_op jit(solution)/shard_map/bgrn,bngd->bgrd/dot_general | solution.py:53
  118.8 2.7 %convolution_convert_fusion = bf16[2,3840]{1,0:T(2,128)(2,1)S(1)} fusion(bf16[2,512]{1,0:T(2,128)(2,1)S(1)} %bitcast.125, bf16[2,512,3840]{2,1,0:T(8,128)(2,1)} %param.23), kind=kOutput, calls=%fused_computation.28 | convolution fusion | flops 7872000 | bytes 3949568 | tf_op jit(solution)/shard_map/dot_general | solution.py:72
  121.5 23.8 %psum.30 = bf16[2,3840]{1,0:T(2,128)(2,1)S(1)} all-reduce(bf16[2,3840]{1,0:T(2,128)(2,1)S(1)} %convolution_convert_fusion), channel_id=1, replica_groups=mesh['dp'=4,'tp'=8] {'tp'}, use_global_device_ids=true, to_apply=%region_11.12 | all-reduce | flops 7680 | bytes 30720 | tf_op jit(solution)/shard_map/psum | solution.py:73
  145.3 0.1 fusion.98
  145.5 0.2 fusion.116
  145.7 6.4 %fusion.135 = f32[2,1920]{1,0:T(2,128)S(1)} fusion(bf16[2,3840,1920]{2,1,0:T(8,128)(2,1)} %param.24, bf16[2,3840]{1,0:T(2,128)(2,1)S(1)} %get-tuple-element.14, f32[2]{0:T(128)S(1)} %add_rsqrt_fusion.1, f32[3840]{0:T(1024)S(1)} %get-tuple-element.12), kind=kOutput, calls=%fused_computation.142 | convolution fusion | flops 29552640 | bytes 14791688 | tf_op jit(solution)/shard_map/dot_general | solution.py:58
  152.1 11.7 %fusion.28 = bf16[2,3840]{1,0:T(2,128)(2,1)S(1)} fusion(bf16[2,1920,3840]{2,1,0:T(8,128)(2,1)} %param.26, f32[2,1920]{1,0:T(2,128)S(1)} %fusion.135, bf16[2,3840,1920]{2,1,0:T(8,128)(2,1)} %param.25, bf16[2,3840]{1,0:T(2,128)(2,1)S(1)} %get-tuple-element.14, f32[2]{0:T(128)S(1)} %add_rsqrt_fusion.1, f32[3840]{0:T(1024)S(1)} %get-tuple-element.12), kind=kOutput, calls=%fused_computation.27 | convolution fusion | flops 59028480 | bytes 29552648 | tf_op jit(solution)/shard_map/dot_general | solution.py:61
  163.8 23.6 %psum.31 = bf16[2,3840]{1,0:T(2,128)(2,1)S(1)} all-reduce(bf16[2,3840]{1,0:T(2,128)(2,1)S(1)} %fusion.28), channel_id=1, replica_groups=mesh['dp'=4,'tp'=8] {'tp'}, use_global_device_ids=true, to_apply=%region_14.15 | all-reduce | flops 7680 | bytes 30720 | tf_op jit(solution)/shard_map/psum | solution.py:76
  187.4 0.1 fusion.101
  187.6 0.7 fusion.119
  (30 shorter events, 0.2 us)
Async XLA Ops:
  8.7 6.3 %copy-start.6 = (bf16[2,3840]{1,0:T(2,128)(2,1)S(1)}, bf16[2,3840]{1,0:T(2,128)(2,1)}, u32[]{:S(2)}) copy-start(bf16[2,3840]{1,0:T(2,128)(2,1)} %param.14) | copy-start | bytes 46084
  8.7 9.7 %copy-start.7 = (s32[2]{0:T(128)S(1)}, s32[2]{0:T(128)}, u32[]{:S(2)}) copy-start(s32[2]{0:T(128)} %param.15) | copy-start | bytes 28
  14.9 5.7 %copy-start.8 = (bf16[2,3840,256]{2,1,0:T(8,128)(2,1)S(1)}, bf16[2,3840,256]{2,1,0:T(8,128)(2,1)}, u32[]{:S(2)}) copy-start(bf16[2,3840,256]{2,1,0:T(8,128)(2,1)} %param.22) | copy-start | bytes 11796484
  14.9 6.1 %copy-start.3 = (bf16[2,1024,1,256]{3,1,2,0:T(8,128)(2,1)S(1)}, bf16[2,1024,1,256]{3,1,2,0:T(8,128)(2,1)}, u32[]{:S(2)}) copy-start(bf16[2,1024,1,256]{3,1,2,0:T(8,128)(2,1)} %param.16) | copy-start | bytes 3145732
  15.0 6.2 %copy-start.4 = (bf16[2,1024,1,256]{3,1,2,0:T(8,128)(2,1)S(1)}, bf16[2,1024,1,256]{3,1,2,0:T(8,128)(2,1)}, u32[]{:S(2)}) copy-start(bf16[2,1024,1,256]{3,1,2,0:T(8,128)(2,1)} %param.17) | copy-start | bytes 3145732
  21.6 34.4 %copy-start.2 = (bf16[2,1024,1,256]{3,1,2,0:T(8,128)(2,1)}, bf16[2,1024,1,256]{3,1,2,0:T(8,128)(2,1)S(1)}, u32[]{:S(2)}) copy-start(bf16[2,1024,1,256]{3,1,2,0:T(8,128)(2,1)S(1)} %get-tuple-element.27) | copy-start | bytes 3145732
  21.6 34.4 %copy-start.5 = (bf16[2,1024,1,256]{3,1,2,0:T(8,128)(2,1)}, bf16[2,1024,1,256]{3,1,2,0:T(8,128)(2,1)S(1)}, u32[]{:S(2)}) copy-start(bf16[2,1024,1,256]{3,1,2,0:T(8,128)(2,1)S(1)} %get-tuple-element.28) | copy-start | bytes 3145732
  98.1 7.6 %copy-start.1 = (bf16[2,4096,1,256]{3,1,2,0:T(8,128)(2,1)S(1)}, bf16[2,4096,1,256]{3,1,2,0:T(8,128)(2,1)}, u32[]{:S(2)}) copy-start(bf16[2,4096,1,256]{3,1,2,0:T(8,128)(2,1)} %param.18) | copy-start | bytes 12582916
  112.4 2.0 %copy-start = (bf16[2,4096,1,256]{3,1,2,0:T(8,128)(2,1)}, bf16[2,4096,1,256]{3,1,2,0:T(8,128)(2,1)S(1)}, u32[]{:S(2)}) copy-start(bf16[2,4096,1,256]{3,1,2,0:T(8,128)(2,1)S(1)} %get-tuple-element.21) | copy-start | bytes 12582916
where the time goes:
time: 191 us; the launch traced here: 188 us
  blocking collectives  95.1 us (50%)
  matrix products  59.4 us (31%)
  local copies, waits for them, and re-layouts  20.3 us (11%)
  other arithmetic  12.8 us (7%)
    psum x2, blocking collectives, decoder_layer(): attn_sum = lax.psum(attn_part.astype(jnp.bfloat16), 'tp')  47.8 us
    psum x2, blocking collectives, decoder_layer(): down_sum = lax.psum(down_part.astype(jnp.bfloat16), 'tp')  47.3 us
    dot_general x2, matrix products, mlp_part(): return jnp.dot(hidden_act, w_down, preferred_element_type=jnp.float32)  23.4 us
    dot_general x3, local copies, waits for them, and re-layouts, project_and_store(): jnp.dot(normed, w_query, preferred_element_type=jnp.float32)  18.2 us
    dot_general x2, matrix products, mlp_part(): gate_proj = jnp.dot(normed, w_gate, preferred_element_type=jnp.float32)  12.7 us
    select_n x2, other arithmetic, project_and_store(): jnp.where(slot_hit, key_new.astype(jnp.bfloat16)[:, None], k_cache)  7.21 us
    dot_general x2, matrix products, project_and_store(): jnp.dot(normed, w_query, preferred_element_type=jnp.float32)  6.74 us
    dot_general x2, matrix products, decoder_layer(): jnp.dot(mixed_heads.reshape(hidden.shape[0], -1), w_out, preferred_elemen...  5.47 us

commit v1 on v0

v1 whole, which is shorter than its diff:
```python
import functools

import jax
import jax.numpy as jnp
from jax import lax
from jax.experimental import pallas as pl
from jax.experimental.pallas import tpu as pltpu
from jax.sharding import PartitionSpec as P

SOFT_CAP = 50.0
NORM_EPS = 1e-6
ROPE_BASE = 10000.0

CHUNK = 256
SLOTS = 18
QKV_PARTS = 5
KV_STEP = 1024

F32 = jnp.float32
BF16 = jnp.bfloat16
MESH = pl.DeviceIdType.MESH


def rms_norm(values, gain_row):
    inv_rms = lax.rsqrt(jnp.mean(values * values, axis=-1, keepdims=True) + NORM_EPS)
    return (values * inv_rms * (1.0 + gain_row)).astype(BF16)


def step_kernel(n_tp, pos_ref, hid_ref, cos_ref, sin_ref, norm_ref, kl_in, vl_in, kg_in, vg_in, wq, wk, wv, wo, wg, wu, wd,
                hid_out, kl, vl, kg, vg,
                ring, bq, bk, bv, x_ref, a_ref, o_ref, h_ref, acc, e_ref, part,
                ring_sem, qkv_sem, cache_sem, send_sem, recv_sem):
    rows, width = hid_ref.shape
    head = kl.shape[2]
    half = head // 2
    ff = wg.shape[2]
    layers = wg.shape[0]
    n_wo = wo.shape[1] // CHUNK
    n_gu = width // CHUNK
    n_dn = ff // CHUNK
    dn_rest = ff - n_dn * CHUNK
    at_gu, at_dn = n_wo, n_wo + n_gu
    per_layer = n_wo + n_gu + n_dn + (1 if dn_rest else 0)
    n_chunks = layers * per_layer
    me = lax.axis_index('tp')

    def chunk_copies(kind, layer, k, slot):
        if kind == 'wo':
            return [pltpu.make_async_copy(wo.at[layer, pl.ds(k * CHUNK, CHUNK)], ring.at[slot], ring_sem.at[slot, 0])]
        if kind == 'gu':
            return [
                pltpu.make_async_copy(wg.at[layer, pl.ds(k * CHUNK, CHUNK)], ring.at[slot, :, pl.ds(0, ff)], ring_sem.at[slot, 0]),
                pltpu.make_async_copy(wu.at[layer, pl.ds(k * CHUNK, CHUNK)], ring.at[slot, :, pl.ds(ff, ff)], ring_sem.at[slot, 1]),
            ]
        if kind == 'dn':
            return [pltpu.make_async_copy(wd.at[layer, pl.ds(k * CHUNK, CHUNK)], ring.at[slot], ring_sem.at[slot, 0])]
        return [pltpu.make_async_copy(wd.at[layer, pl.ds(n_dn * CHUNK, dn_rest)], ring.at[slot, pl.ds(0, dn_rest)], ring_sem.at[slot, 0])]

    def start_chunk(c):
        slot = lax.rem(c, SLOTS)
        layer = c // per_layer
        r = c - layer * per_layer

        def go(kind, k):
            for copy in chunk_copies(kind, layer, k, slot):
                copy.start()

        if isinstance(c, int):
            if r < at_gu:
                go('wo', r)
            elif r < at_dn:
                go('gu', r - at_gu)
            elif r < at_dn + n_dn:
                go('dn', r - at_dn)
            else:
                go('rest', 0)
            return
        live = c < n_chunks
        pl.when(live & (r < at_gu))(lambda: go('wo', r))
        pl.when(live & (r >= at_gu) & (r < at_dn))(lambda: go('gu', r - at_gu))
        pl.when(live & (r >= at_dn) & (r < at_dn + n_dn))(lambda: go('dn', r - at_dn))
        if dn_rest:
            pl.when(live & (r == at_dn + n_dn))(lambda: go('rest', 0))

    def stream_dot(kind, layer, lhs_ref, first, count):
        def body(k, carry):
            c = layer * per_layer + first + k
            slot = lax.rem(c, SLOTS)
            for copy in chunk_copies(kind, layer, k, slot):
                copy.wait()
            lhs = lhs_ref[:, pl.ds(pl.multiple_of(k * CHUNK, CHUNK), CHUNK)]
            acc[...] += jnp.dot(lhs, ring[slot], preferred_element_type=F32)
            start_chunk(c + SLOTS)
            return carry

        lax.fori_loop(0, count, body, 0)

    qkv_rows = width // QKV_PARTS

    def qkv_copies(layer, j):
        piece = pl.ds(j * qkv_rows, qkv_rows)
        return [pltpu.make_async_copy(src.at[layer, piece], dst.at[piece], qkv_sem.at[i, j])
                for i, (src, dst) in enumerate(((wq, bq), (wk, bk), (wv, bv)))]

    def cache_copies(layer):
        pairs = ((kl_in, kl), (vl_in, vl)) if layer == 0 else ((kg_in, kg), (vg_in, vg))
        return [pltpu.make_async_copy(src.at[b], dst.at[b], cache_sem.at[layer, i, b])
                for i, (src, dst) in enumerate(pairs) for b in range(rows)]

    def send_copies(phase):
        copies = []
        for step in range(1, n_tp):
            peer = lax.rem(me + step, n_tp)
            copies.append(pltpu.make_async_remote_copy(
                src_ref=part.at[phase, me], dst_ref=part.at[phase, me],
                send_sem=send_sem.at[phase, step - 1], recv_sem=recv_sem.at[phase, step - 1],
                device_id={'tp': peer}, device_id_type=MESH))
        return copies

    def exchange(phase):
        part[phase, me] = acc[...].astype(BF16)
        copies = send_copies(phase)
        for copy in copies:
            copy.start()
        for copy in copies:
            copy.wait_recv()
        total = part[phase, 0].astype(F32)
        for j in range(1, n_tp):
            total = total + part[phase, j].astype(F32)
        return total

    def gain(layer, i):
        return norm_ref[layer, pl.ds(i, 1), :]

    def add_normed(layer, i, branch_sum):
        x = (x_ref[...] + rms_norm(branch_sum, gain(layer, i)).astype(F32)).astype(BF16)
        x_ref[...] = x.astype(F32)
        return x

    def rotate(values):
        first, second = values[:, :half], values[:, half:]
        cos_part, sin_part = cos_ref[...], sin_ref[...]
        return jnp.concatenate([first * cos_part - second * sin_part, second * cos_part + first * sin_part], axis=-1)

    def store_row(cache, b, slot, new_row):
        n = cache.shape[1]
        step = min(n, KV_STEP)

        def body(i, carry):
            piece = pl.ds(pl.multiple_of(i * step, step), step)
            ids = lax.broadcasted_iota(jnp.int32, (step, head), 0) + i * step
            cache[b, piece] = jnp.where(ids == slot, jnp.broadcast_to(new_row, (step, head)), cache[b, piece])
            return carry

        lax.fori_loop(0, n // step, body, 0)

    def attention(layer, kc, vc):
        n = kc.shape[1]
        a_ref[...] = rms_norm(x_ref[...], gain(layer, 0))
        hq = bq.shape[1]

        def qkv_body(j, carry):
            q, k, v = carry
            for copy in qkv_copies(layer, j):
                copy.wait()
            piece = pl.ds(pl.multiple_of(j * qkv_rows, qkv_rows), qkv_rows)
            lhs = a_ref[:, piece]
            q = q + jnp.dot(lhs, bq[piece], preferred_element_type=F32)
            k = k + jnp.dot(lhs, bk[piece], preferred_element_type=F32)
            v = v + jnp.dot(lhs, bv[piece], preferred_element_type=F32)
            return q, k, v

        q, k, v = lax.fori_loop(0, QKV_PARTS, qkv_body, (
            jnp.zeros((rows, hq), F32), jnp.zeros((rows, head), F32), jnp.zeros((rows, head), F32)))
        if layer + 1 < layers:
            for j in range(QKV_PARTS):
                for copy in qkv_copies(layer + 1, j):
                    copy.start()
        group = hq // head
        queries = jnp.concatenate([rotate(q[:, g * head:(g + 1) * head]) for g in range(group)], axis=0).astype(BF16)
        k_new = rotate(k).astype(BF16)
        v_new = v.astype(BF16)
        for copy in cache_copies(layer):
            copy.wait()
        for b in range(rows):
            slot = lax.rem(pos_ref[b], n)
            store_row(kc, b, slot, k_new[b:b + 1])
            store_row(vc, b, slot, v_new[b:b + 1])
        q_rows = group * rows
        row_seq = lax.rem(lax.broadcasted_iota(jnp.int32, (q_rows, 1), 0), rows)
        last = jnp.zeros((q_rows, 1), jnp.int32)
        for b in range(rows):
            last = jnp.where(row_seq == b, pos_ref[b], last)

        def pick(per_seq):
            out = per_seq[0]
            for b in range(1, rows):
                out = jnp.where(row_seq == b, per_seq[b], out)
            return out

        step = min(n, KV_STEP)
        contract_last = (((1,), (1,)), ((), ()))

        def score_body(i, total):
            piece = pl.ds(pl.multiple_of(i * step, step), step)
            s = pick([lax.dot_general(queries, kc[b, piece], contract_last, preferred_element_type=F32) for b in range(rows)])
            s = s * head ** -0.5
            e = jnp.exp(SOFT_CAP * jnp.tanh(s / SOFT_CAP))
            ids = lax.broadcasted_iota(jnp.int32, (q_rows, step), 1) + i * step
            e = jnp.where(ids <= last, e, 0.0)
            e_ref[:, piece] = e
            return total + jnp.sum(e, axis=-1, keepdims=True)

        total = lax.fori_loop(0, n // step, score_body, jnp.zeros((q_rows, 1), F32))

        def value_body(i, out):
            piece = pl.ds(pl.multiple_of(i * step, step), step)
            probs = (e_ref[:, piece] / total).astype(BF16)
            return out + pick([jnp.dot(probs, vc[b, piece], preferred_element_type=F32) for b in range(rows)])

        mixed = lax.fori_loop(0, n // step, value_body, jnp.zeros((q_rows, head), F32)).astype(BF16)
        for g in range(group):
            o_ref[:, pl.ds(g * head, head)] = mixed[g * rows:(g + 1) * rows]

    for j in range(QKV_PARTS):
        for copy in qkv_copies(0, j):
            copy.start()
    for copy in cache_copies(0):
        copy.start()
    for c in range(min(SLOTS, n_chunks)):
        start_chunk(c)
    for copy in cache_copies(1):
        copy.start()

    barrier = pltpu.get_barrier_semaphore()
    for step in range(1, n_tp):
        pl.semaphore_signal(barrier, inc=1, device_id={'tp': lax.rem(me + step, n_tp)}, device_id_type=MESH)

    x_ref[...] = hid_ref[...].astype(F32)
    for layer in range(layers):
        kc, vc = (kl, vl) if layer == 0 else (kg, vg)
        attention(layer, kc, vc)
        acc[...] = jnp.zeros_like(acc)
        stream_dot('wo', layer, o_ref, 0, n_wo)
        if layer == 0:
            pl.semaphore_wait(barrier, n_tp - 1)
        x = add_normed(layer, 1, exchange(2 * layer))
        a_ref[...] = rms_norm(x.astype(F32), gain(layer, 2))
        acc[...] = jnp.zeros_like(acc)
        stream_dot('gu', layer, a_ref, at_gu, n_gu)
        gate_up = acc[...]
        h_ref[...] = (jax.nn.gelu(gate_up[:, :ff], approximate=True) * gate_up[:, ff:]).astype(BF16)
        acc[...] = jnp.zeros_like(acc)
        stream_dot('dn', layer, h_ref, at_dn, n_dn)
        if dn_rest:
            c = layer * per_layer + per_layer - 1
            slot = c % SLOTS
            for copy in chunk_copies('rest', layer, 0, slot):
                copy.wait()
            acc[...] += jnp.dot(h_ref[:, pl.ds(n_dn * CHUNK, dn_rest)], ring[slot, pl.ds(0, dn_rest)], preferred_element_type=F32)
            if c + SLOTS < n_chunks:
                start_chunk(c + SLOTS)
        x = add_normed(layer, 3, exchange(2 * layer + 1))
    hid_out[...] = x
    for phase in range(2 * layers):
        for copy in send_copies(phase):
            copy.wait_send()


def decode_step(n_tp, hidden, positions, k_local, v_local, k_global, v_global, w_query, w_key, w_value, w_out, w_gate, w_up, w_down, norm_scale):
    rows, width = hidden.shape
    caches = [c.reshape(c.shape[0], c.shape[1], c.shape[3]) for c in (k_local, v_local, k_global, v_global)]
    head = caches[0].shape[2]
    half = head // 2
    inv_freq = ROPE_BASE ** (-2.0 * jnp.arange(half, dtype=F32) / head)
    angles = positions.astype(F32)[:, None] * inv_freq
    cos_part, sin_part = jnp.cos(angles), jnp.sin(angles)
    hq, ff, layers = w_query.shape[2], w_gate.shape[2], w_gate.shape[0]
    n_ctx = max(c.shape[1] for c in caches)
    vmem = pl.BlockSpec(memory_space=pltpu.VMEM)
    hbm = pl.BlockSpec(memory_space=pl.ANY)
    smem = pl.BlockSpec(memory_space=pltpu.SMEM)
    outs = pl.pallas_call(
        functools.partial(step_kernel, n_tp),
        out_shape=(jax.ShapeDtypeStruct(hidden.shape, BF16),) + tuple(jax.ShapeDtypeStruct(c.shape, BF16) for c in caches),
        in_specs=[smem] + [vmem] * 4 + [hbm] * 11,
        out_specs=(vmem,) * 5,
        scratch_shapes=[
            pltpu.VMEM((SLOTS, CHUNK, width), BF16),
            pltpu.VMEM((width, hq), BF16),
            pltpu.VMEM((width, head), BF16),
            pltpu.VMEM((width, head), BF16),
            pltpu.VMEM((rows, width), F32),
            pltpu.VMEM((rows, width), BF16),
            pltpu.VMEM((rows, hq), BF16),
            pltpu.VMEM((rows, ff), BF16),
            pltpu.VMEM((rows, 2 * ff), F32),
            pltpu.VMEM((hq // head * rows, n_ctx), F32),
            pltpu.VMEM((2 * layers, n_tp, rows, width), BF16),
            pltpu.SemaphoreType.DMA((SLOTS, 2)),
            pltpu.SemaphoreType.DMA((3, QKV_PARTS)),
            pltpu.SemaphoreType.DMA((2, 2, rows)),
            pltpu.SemaphoreType.DMA((2 * layers, n_tp - 1)),
            pltpu.SemaphoreType.DMA((2 * layers, n_tp - 1)),
        ],
        compiler_params=pltpu.CompilerParams(
            collective_id=0, has_side_effects=True, vmem_limit_bytes=56 * 1024 * 1024),
        name='decode_step',
    )(positions, hidden, cos_part, sin_part, norm_scale, *caches, w_query, w_key, w_value, w_out, w_gate, w_up, w_down)
    hidden_out = outs[0]
    new_caches = [c.reshape(old.shape) for c, old in zip(outs[1:], (k_local, v_local, k_global, v_global))]
    return (hidden_out, *new_caches)


def solution(mesh):
    row_spec = P('dp', None)
    cache_spec = P('dp', None, 'tp', None)
    col_split = P(None, None, 'tp')
    row_split = P(None, 'tp', None)
    in_specs = (row_spec, P('dp'), cache_spec, cache_spec, cache_spec, cache_spec, col_split, col_split, col_split, row_split, col_split, col_split, row_split, P())
    out_specs = (row_spec, cache_spec, cache_spec, cache_spec, cache_spec)
    return jax.shard_map(functools.partial(decode_step, mesh.shape['tp']), mesh=mesh, in_specs=in_specs, out_specs=out_specs, check_vma=False)
```

time: 191 us -> 81 us (0.42); the launches traced: 188 us -> 80.8 us
  blocking collectives: 95.1 us -> 0 us
  Pallas kernels: 0 us -> 67.1 us
  matrix products: 59.4 us -> 0 us
  other arithmetic: 12.8 us -> 1.35 us
  local copies, waits for them, and re-layouts: 20.3 us -> 11.7 us
    psum x4 -> x0, blocking collectives: 95.1 us -> none  [the longest x2 47.8 us: decoder_layer(): attn_sum = lax.psum(attn_part.astype(jnp.bfloat16), 'tp')]
    pallas_call x0 -> x1, Pallas kernels: none -> 67.1 us  [decode_step(): pl.pallas_call(functools.partial(step_kernel, n_tp), out_shape=(jax.Shape...]
    dot_general x16 -> x0, matrix products: 59.4 us -> none  [the longest x2 23.4 us: mlp_part(): return jnp.dot(hidden_act, w_down, preferred_element_type=jnp.float32)]
    dot_general x3 -> x0, local copies, waits for them, and re-layouts: 18.2 us -> none  [project_and_store(): jnp.dot(normed, w_query, preferred_element_type=jnp.float32)]
    unnamed x20 -> x9, local copies, waits for them, and re-layouts: 2.06 us -> 11.7 us
    select_n x2 -> x0, other arithmetic: 7.21 us -> none  [project_and_store(): jnp.where(slot_hit, key_new.astype(jnp.bfloat16)[:, None], k_cache)]
    reduce_sum x8 -> x0, other arithmetic: 2.1 us -> none  [rms_norm(): jnp.mean(values_f32 * values_f32, axis=-1, keepdims=True) + NORM_EPS]
where the time goes in v1:
time: 81 us; the launch traced here: 80.8 us
  Pallas kernels  67.1 us (83%)
  local copies, waits for them, and re-layouts  11.7 us (14%)
  other arithmetic  1.35 us (2%)
    pallas_call x1, Pallas kernels, decode_step(): pl.pallas_call(functools.partial(step_kernel, n_tp), out_shape=(jax.Shape...  67.1 us
    unnamed x9, local copies, waits for them, and re-layouts  11.7 us

profile of v1, /device:TPU:81, one launch (start us, length us, event | category | flops | bytes accessed | tf_op | source)
XLA Modules:
  0.0 80.8 jit_solution(11918645935193428010)
XLA Ops:
  0.6 0.7 convert_element_type.3
  1.3 0.7 multiply_sine_fusion
  2.0 67.1 %decode_step.1 = (bf16[2,3840]{1,0:T(2,128)(2,1)}, bf16[2,1024,256]{2,1,0:T(8,128)(2,1)}, bf16[2,1024,256]{2,1,0:T(8,128)(2,1)}, bf16[2,4096,256]{2,1,0:T(8,128)(2,1)}, bf16[2,4096,256]{2,1,0:T(8,128)(2,1)}) custom-call(s32[2]{0:T(128)} %pos_ref.1, bf16[2,3840]{1,0:T(2,128)(2,1)} %hid_ref.1, f32[2,128]{1,0:T(2,128)} %get-tuple-element.21.cos_ref, ...), custom_call_target="tpu_custom_call" | custom-call | tf_op jit(solution)/shard_map/decode_step/pallas_call | solution.py:283
  69.1 0.0 copy-start.1
  69.1 1.5 %copy.28 = bf16[2,3840]{1,0:T(2,128)(2,1)} copy(bf16[2,3840]{1,0:T(2,128)(2,1)} %get-tuple-element.27) | data formatting | bytes 30720
  70.6 2.3 %copy.29 = bf16[2,1024,1,256]{3,1,2,0:T(8,128)(2,1)} copy(bf16[2,1024,1,256]{3,1,2,0:T(8,128)(2,1)} %bitcast.23) | data formatting | bytes 2097152
  72.8 2.3 %copy.30 = bf16[2,1024,1,256]{3,1,2,0:T(8,128)(2,1)} copy(bf16[2,1024,1,256]{3,1,2,0:T(8,128)(2,1)} %bitcast.22) | data formatting | bytes 2097152
  75.1 0.0 copy-done.1
  75.1 0.0 copy-start
  75.1 2.1 %copy.31 = bf16[2,4096,1,256]{3,1,2,0:T(8,128)(2,1)} copy(bf16[2,4096,1,256]{3,1,2,0:T(8,128)(2,1)S(1)} %bitcast.19) | data formatting | bytes 8388608
  77.2 1.6 %copy-done = bf16[2,4096,256]{2,1,0:T(8,128)(2,1)S(1)} copy-done((bf16[2,4096,256]{2,1,0:T(8,128)(2,1)S(1)}, bf16[2,4096,256]{2,1,0:T(8,128)(2,1)}, u32[]{:S(2)}) %copy-start) | copy-done | bytes 4194328
  78.8 2.0 %copy.32 = bf16[2,4096,1,256]{3,1,2,0:T(8,128)(2,1)} copy(bf16[2,4096,1,256]{3,1,2,0:T(8,128)(2,1)S(1)} %bitcast.18) | data formatting | bytes 8388608
  (1 shorter events, 0.0 us)
Async XLA Ops:
  69.1 6.0 %copy-start.1 = (bf16[2,4096,256]{2,1,0:T(8,128)(2,1)S(1)}, bf16[2,4096,256]{2,1,0:T(8,128)(2,1)}, u32[]{:S(2)}) copy-start(bf16[2,4096,256]{2,1,0:T(8,128)(2,1)} %get-tuple-element.13) | copy-start | bytes 12582916
  75.1 3.7 %copy-start = (bf16[2,4096,256]{2,1,0:T(8,128)(2,1)S(1)}, bf16[2,4096,256]{2,1,0:T(8,128)(2,1)}, u32[]{:S(2)}) copy-start(bf16[2,4096,256]{2,1,0:T(8,128)(2,1)} %get-tuple-element.14) | copy-start | bytes 12582916

commit v2 on v1

v2 whole, which is shorter than its diff:
```python
import functools

import jax
import jax.numpy as jnp
import numpy as np
from jax import lax
from jax.experimental import pallas as pl
from jax.experimental.pallas import tpu as pltpu
from jax.sharding import PartitionSpec as P

SOFT_CAP = 50.0
NORM_EPS = 1e-6
ROPE_BASE = 10000.0

CHUNK = 256
SLOTS = 22
QKV_PARTS = 5
KV_STEP = 1024
GU_GROUP = 5
DN_GROUP = 3

VMEM_LIMIT = 52 * 1024 * 1024

F32 = jnp.float32
BF16 = jnp.bfloat16
MESH = pl.DeviceIdType.MESH


def rem(a, b):
    return a % b if isinstance(a, int) else lax.rem(a, b)


def rms_norm(values, gain_row):
    inv_rms = lax.rsqrt(jnp.mean(values * values, axis=-1, keepdims=True) + NORM_EPS)
    return (values * inv_rms * (1.0 + gain_row)).astype(BF16)


def step_kernel(n_tp, pos_in, hid_in, freq_in, norm_in, kl_in, vl_in, kg_in, vg_in, wq, wk, wv, wo, wg, wu, wd,
                hid_out, kl, vl, kg, vg,
                pos_ref, hid_ref, freq_ref, norm_ref, ring, bq, bk, bv, x_ref, a_ref, o_ref, h_ref, acc, e_ref, part,
                small_sem, ring_sem, qkv_sem, cache_sem, send_sem, recv_sem):
    rows, width = hid_ref.shape
    head = kl.shape[2]
    half = head // 2
    ff = wg.shape[2]
    layers = wg.shape[0]
    n_wo = wo.shape[1] // CHUNK
    n_gu = width // CHUNK
    n_dn = ff // CHUNK
    dn_rest = ff - n_dn * CHUNK
    at_gu, at_dn = n_wo, n_wo + n_gu
    per_layer = n_wo + n_gu + n_dn + (1 if dn_rest else 0)
    n_chunks = layers * per_layer
    me = lax.axis_index('tp')

    def chunk_copies(kind, layer, k, slot):
        if kind == 'wo':
            return [pltpu.make_async_copy(wo.at[layer, pl.ds(k * CHUNK, CHUNK)], ring.at[slot], ring_sem.at[slot, 0])]
        if kind == 'gu':
            return [
                pltpu.make_async_copy(wg.at[layer, pl.ds(k * CHUNK, CHUNK)], ring.at[slot, :, pl.ds(0, ff)], ring_sem.at[slot, 0]),
                pltpu.make_async_copy(wu.at[layer, pl.ds(k * CHUNK, CHUNK)], ring.at[slot, :, pl.ds(ff, ff)], ring_sem.at[slot, 1]),
            ]
        if kind == 'dn':
            return [pltpu.make_async_copy(wd.at[layer, pl.ds(k * CHUNK, CHUNK)], ring.at[slot], ring_sem.at[slot, 0])]
        return [pltpu.make_async_copy(wd.at[layer, pl.ds(n_dn * CHUNK, dn_rest)], ring.at[slot, pl.ds(0, dn_rest)], ring_sem.at[slot, 0])]

    def start_chunk(c):
        slot = rem(c, SLOTS)
        layer = c // per_layer
        r = c - layer * per_layer

        def go(kind, k):
            for copy in chunk_copies(kind, layer, k, slot):
                copy.start()

        if isinstance(c, int):
            if c >= n_chunks:
                return
            if r < at_gu:
                go('wo', r)
            elif r < at_dn:
                go('gu', r - at_gu)
            elif r < at_dn + n_dn:
                go('dn', r - at_dn)
            else:
                go('rest', 0)
            return
        live = c < n_chunks
        pl.when(live & (r < at_gu))(lambda: go('wo', r))
        pl.when(live & (r >= at_gu) & (r < at_dn))(lambda: go('gu', r - at_gu))
        pl.when(live & (r >= at_dn) & (r < at_dn + n_dn))(lambda: go('dn', r - at_dn))
        if dn_rest:
            pl.when(live & (r == at_dn + n_dn))(lambda: go('rest', 0))

    def group_dot(kind, layer, lhs_ref, first, k0, group, rest=False):
        base = layer * per_layer + first + k0
        slots = [rem(base + j, SLOTS) for j in range(group)]
        for j, slot in enumerate(slots):
            for copy in chunk_copies(kind, layer, k0 + j, slot):
                copy.wait()
        out = acc[...]
        if rest:
            rest_slot = rem(base + group, SLOTS)
            for copy in chunk_copies('rest', layer, 0, rest_slot):
                copy.wait()
        for j, slot in enumerate(slots):
            at = (k0 + j) * CHUNK
            lhs = lhs_ref[:, pl.ds(at if isinstance(at, int) else pl.multiple_of(at, CHUNK), CHUNK)]
            out = out + jnp.dot(lhs, ring[slot], preferred_element_type=F32)
        if rest:
            out = out + jnp.dot(lhs_ref[:, pl.ds(n_dn * CHUNK, dn_rest)], ring[rest_slot, pl.ds(0, dn_rest)], preferred_element_type=F32)
        acc[...] = out
        for j in range(group + (1 if rest else 0)):
            start_chunk(base + j + SLOTS)

    def stream_dot(kind, layer, lhs_ref, first, count, group, rest=False):
        acc[...] = jnp.zeros_like(acc)
        steps, left = divmod(count, group)
        if rest and not left:
            steps, left = steps - 1, group

        def body(i, carry):
            group_dot(kind, layer, lhs_ref, first, i * group, group)
            return carry

        if steps == 1:
            body(0, 0)
        else:
            lax.fori_loop(0, steps, body, 0)
        if left or rest:
            group_dot(kind, layer, lhs_ref, first, steps * group, left, rest)

    qkv_rows = width // QKV_PARTS

    def qkv_copies(layer, j):
        piece = pl.ds(j * qkv_rows, qkv_rows)
        return [pltpu.make_async_copy(src.at[layer, piece], dst.at[piece], qkv_sem.at[i, j])
                for i, (src, dst) in enumerate(((wq, bq), (wk, bk), (wv, bv)))]

    def cache_copies(layer):
        pairs = ((kl_in, kl), (vl_in, vl)) if layer == 0 else ((kg_in, kg), (vg_in, vg))
        return [pltpu.make_async_copy(src.at[b], dst.at[b], cache_sem.at[layer, i, b])
                for i, (src, dst) in enumerate(pairs) for b in range(rows)]

    def send_copies(phase):
        copies = []
        for step in range(1, n_tp):
            peer = lax.rem(me + step, n_tp)
            copies.append(pltpu.make_async_remote_copy(
                src_ref=part.at[phase, me], dst_ref=part.at[phase, me],
                send_sem=send_sem.at[phase, step - 1], recv_sem=recv_sem.at[phase, step - 1],
                device_id={'tp': peer}, device_id_type=MESH))
        return copies

    def exchange(phase, meanwhile=None):
        part[phase, me] = acc[...].astype(BF16)
        copies = send_copies(phase)
        for copy in copies:
            copy.start()
        if meanwhile is not None:
            meanwhile()
        for copy in copies:
            copy.wait_recv()
        total = part[phase, 0].astype(F32)
        for j in range(1, n_tp):
            total = total + part[phase, j].astype(F32)
        return total

    def gain(layer, i):
        return norm_ref[layer, pl.ds(i, 1), :]

    def add_normed(layer, i, branch_sum):
        x = (x_ref[...] + rms_norm(branch_sum, gain(layer, i)).astype(F32)).astype(BF16)
        x_ref[...] = x.astype(F32)
        return x

    def rotate(values, trig):
        first, second = values[:, :half], values[:, half:]
        cos_part, sin_part = trig
        return jnp.concatenate([first * cos_part - second * sin_part, second * cos_part + first * sin_part], axis=-1)

    def store_row(cache, b, slot, new_row):
        n = cache.shape[1]
        step = min(n, KV_STEP)

        def body(i, carry):
            piece = pl.ds(pl.multiple_of(i * step, step), step)
            ids = lax.broadcasted_iota(jnp.int32, (step, head), 0) + i * step
            cache[b, piece] = jnp.where(ids == slot, jnp.broadcast_to(new_row, (step, head)), cache[b, piece])
            return carry

        lax.fori_loop(0, n // step, body, 0)

    def attention(layer, kc, vc, trig):
        n = kc.shape[1]
        a_ref[...] = rms_norm(x_ref[...], gain(layer, 0))
        hq = bq.shape[1]

        q, k, v = jnp.zeros((rows, hq), F32), jnp.zeros((rows, head), F32), jnp.zeros((rows, head), F32)
        if layer > 0:
            for j in range(QKV_PARTS):
                for copy in qkv_copies(layer, j):
                    copy.wait()
        for j in range(QKV_PARTS):
            if layer == 0:
                for copy in qkv_copies(layer, j):
                    copy.wait()
            piece = pl.ds(j * qkv_rows, qkv_rows)
            lhs = a_ref[:, piece]
            q = q + jnp.dot(lhs, bq[piece], preferred_element_type=F32)
            k = k + jnp.dot(lhs, bk[piece], preferred_element_type=F32)
            v = v + jnp.dot(lhs, bv[piece], preferred_element_type=F32)
        if layer + 1 < layers:
            for j in range(QKV_PARTS):
                for copy in qkv_copies(layer + 1, j):
                    copy.start()
        group = hq // head
        queries = jnp.concatenate([rotate(q[:, g * head:(g + 1) * head], trig) for g in range(group)], axis=0).astype(BF16)
        k_new = rotate(k, trig).astype(BF16)
        v_new = v.astype(BF16)
        for copy in cache_copies(layer):
            copy.wait()
        q_rows = group * rows
        row_seq = lax.rem(lax.broadcasted_iota(jnp.int32, (q_rows, 1), 0), rows)
        last, slot = jnp.zeros((q_rows, 1), jnp.int32), jnp.zeros((q_rows, 1), jnp.int32)
        for b in range(rows):
            last = jnp.where(row_seq == b, pos_ref[b], last)
            slot = jnp.where(row_seq == b, lax.rem(pos_ref[b], n), slot)

        def pick(per_seq):
            out = per_seq[0]
            for b in range(1, rows):
                out = jnp.where(row_seq == b, per_seq[b], out)
            return out

        step = min(n, KV_STEP)
        contract_last = (((1,), (1,)), ((), ()))

        def soft_exp(s):
            return jnp.exp(SOFT_CAP * jnp.tanh(s * head ** -0.5 / SOFT_CAP))

        per_row = [jnp.concatenate([new.astype(F32)] * group, axis=0) for new in (k_new, v_new)]
        e_new = soft_exp(jnp.sum(queries.astype(F32) * per_row[0], axis=-1, keepdims=True))
        total = e_new
        weights = []
        for i in range(n // step):
            piece = pl.ds(i * step, step)
            s = pick([lax.dot_general(queries, kc[b, piece], contract_last, preferred_element_type=F32) for b in range(rows)])
            ids = lax.broadcasted_iota(jnp.int32, (q_rows, step), 1) + i * step
            e = jnp.where((ids <= last) & (ids != slot), soft_exp(s), 0.0)
            e_ref[:, piece] = e
            total = total + jnp.sum(e, axis=-1, keepdims=True)
        out = (e_new / total).astype(BF16).astype(F32) * per_row[1]
        for i in range(n // step):
            piece = pl.ds(i * step, step)
            probs = (e_ref[:, piece] / total).astype(BF16)
            out = out + pick([jnp.dot(probs, vc[b, piece], preferred_element_type=F32) for b in range(rows)])
        mixed = out.astype(BF16)
        for g in range(group):
            o_ref[:, pl.ds(g * head, head)] = mixed[g * rows:(g + 1) * rows]

        def store_new():
            for b in range(rows):
                store_row(kc, b, lax.rem(pos_ref[b], n), k_new[b:b + 1])
                store_row(vc, b, lax.rem(pos_ref[b], n), v_new[b:b + 1])

        return store_new

    small = [pltpu.make_async_copy(src, dst, small_sem.at[i]) for i, (src, dst) in enumerate(
        ((hid_in, hid_ref), (norm_in, norm_ref), (pos_in, pos_ref), (freq_in, freq_ref)))]
    for copy in small:
        copy.start()
    for j in range(QKV_PARTS):
        for copy in qkv_copies(0, j):
            copy.start()
    for copy in cache_copies(0):
        copy.start()
    for c in range(min(SLOTS, n_chunks)):
        start_chunk(c)
    for copy in cache_copies(1):
        copy.start()

    barrier = pltpu.get_barrier_semaphore()
    for step in range(1, n_tp):
        pl.semaphore_signal(barrier, inc=1, device_id={'tp': lax.rem(me + step, n_tp)}, device_id_type=MESH)

    for copy in small:
        copy.wait()
    x_ref[...] = hid_ref[...].astype(F32)
    row_ids = lax.broadcasted_iota(jnp.int32, (rows, half), 0)
    pos_rows = jnp.zeros((rows, half), F32)
    for b in range(rows):
        pos_rows = jnp.where(row_ids == b, pos_ref[b].astype(F32), pos_rows)
    angles = pos_rows * freq_ref[...]
    trig = jnp.cos(angles), jnp.sin(angles)
    for layer in range(layers):
        kc, vc = (kl, vl) if layer == 0 else (kg, vg)
        store_new = attention(layer, kc, vc, trig)
        stream_dot('wo', layer, o_ref, 0, n_wo, n_wo)
        if layer == 0:
            pl.semaphore_wait(barrier, n_tp - 1)
        x = add_normed(layer, 1, exchange(2 * layer, store_new))
        a_ref[...] = rms_norm(x.astype(F32), gain(layer, 2))
        stream_dot('gu', layer, a_ref, at_gu, n_gu, GU_GROUP)
        gate_up = acc[...]
        h_ref[...] = (jax.nn.gelu(gate_up[:, :ff], approximate=True) * gate_up[:, ff:]).astype(BF16)
        stream_dot('dn', layer, h_ref, at_dn, n_dn, DN_GROUP, dn_rest > 0)
        x = add_normed(layer, 3, exchange(2 * layer + 1))
    hid_out[...] = x
    for phase in range(2 * layers):
        for copy in send_copies(phase):
            copy.wait_send()


def write_kernel(*refs):
    n = len(refs) // 2
    copies = [pltpu.make_async_copy(refs[i], refs[n + i], refs[-1].at[i]) for i in range(n)]
    for copy in copies:
        copy.start()
    for copy in copies:
        copy.wait()


def decode_step(n_tp, hidden, positions, k_local, v_local, k_global, v_global, w_query, w_key, w_value, w_out, w_gate, w_up, w_down, norm_scale):
    rows, width = hidden.shape
    caches = [c.reshape(c.shape[0], c.shape[1], c.shape[3]) for c in (k_local, v_local, k_global, v_global)]
    head = caches[0].shape[2]
    half = head // 2
    inv_freq = jnp.asarray(ROPE_BASE ** (-2.0 * np.arange(half) / head), F32)[None, :]
    hq, ff, layers = w_query.shape[2], w_gate.shape[2], w_gate.shape[0]
    n_ctx = max(c.shape[1] for c in caches)
    vmem = pl.BlockSpec(memory_space=pltpu.VMEM)
    hbm = pl.BlockSpec(memory_space=pl.ANY)
    outs = pl.pallas_call(
        functools.partial(step_kernel, n_tp),
        out_shape=tuple(pltpu.VMEM(a.shape, BF16) for a in (hidden, *caches)),
        in_specs=[hbm] * 15,
        out_specs=(vmem,) * 5,
        scratch_shapes=[
            pltpu.SMEM((rows,), jnp.int32),
            pltpu.VMEM((rows, width), BF16),
            pltpu.VMEM((1, half), F32),
            pltpu.VMEM(norm_scale.shape, F32),
            pltpu.VMEM((SLOTS, CHUNK, width), BF16),
            pltpu.VMEM((width, hq), BF16),
            pltpu.VMEM((width, head), BF16),
            pltpu.VMEM((width, head), BF16),
            pltpu.VMEM((rows, width), F32),
            pltpu.VMEM((rows, width), BF16),
            pltpu.VMEM((rows, hq), BF16),
            pltpu.VMEM((rows, ff), BF16),
            pltpu.VMEM((rows, 2 * ff), F32),
            pltpu.VMEM((hq // head * rows, n_ctx), F32),
            pltpu.VMEM((2 * layers, n_tp, rows, width), BF16),
            pltpu.SemaphoreType.DMA((4,)),
            pltpu.SemaphoreType.DMA((SLOTS, 2)),
            pltpu.SemaphoreType.DMA((3, QKV_PARTS)),
            pltpu.SemaphoreType.DMA((2, 2, rows)),
            pltpu.SemaphoreType.DMA((2 * layers, n_tp - 1)),
            pltpu.SemaphoreType.DMA((2 * layers, n_tp - 1)),
        ],
        compiler_params=pltpu.CompilerParams(
            collective_id=0, has_side_effects=True, vmem_limit_bytes=VMEM_LIMIT),
        name='decode_step',
    )(positions, hidden, inv_freq, norm_scale, *caches, w_query, w_key, w_value, w_out, w_gate, w_up, w_down)
    hidden_out, *new_caches = pl.pallas_call(
        write_kernel,
        out_shape=tuple(jax.ShapeDtypeStruct(o.shape, o.dtype) for o in outs),
        in_specs=[hbm] * len(outs),
        out_specs=(hbm,) * len(outs),
        scratch_shapes=[pltpu.SemaphoreType.DMA((len(outs),))],
        compiler_params=pltpu.CompilerParams(vmem_limit_bytes=1024 * 1024),
        name='write_out',
    )(*outs)
    new_caches = [c.reshape(old.shape) for c, old in zip(new_caches, (k_local, v_local, k_global, v_global))]
    return (hidden_out, *new_caches)


def solution(mesh):
    row_spec = P('dp', None)
    cache_spec = P('dp', None, 'tp', None)
    col_split = P(None, None, 'tp')
    row_split = P(None, 'tp', None)
    in_specs = (row_spec, P('dp'), cache_spec, cache_spec, cache_spec, cache_spec, col_split, col_split, col_split, row_split, col_split, col_split, row_split, P())
    out_specs = (row_spec, cache_spec, cache_spec, cache_spec, cache_spec)
    return jax.shard_map(functools.partial(decode_step, mesh.shape['tp']), mesh=mesh, in_specs=in_specs, out_specs=out_specs, check_vma=False)
```

time: 81 us -> 62.3 us (0.77)
  local copies, waits for them, and re-layouts: 11.7 us -> 0 us
  Pallas kernels: 67.1 us -> 61.6 us
  other arithmetic: 1.35 us -> 0 us
    unnamed x9 -> x0, local copies, waits for them, and re-layouts: 11.7 us -> none
    pallas_call x1 -> x2, Pallas kernels: 67.1 us -> 61.6 us  [the longest x1 57.4 us: decode_step(): pl.pallas_call(functools.partial(step_kernel, n_tp), out_shape=tuple((plt...]
where the time goes in v2:
time: 62.3 us; the launch traced here: 62.2 us
  Pallas kernels  61.6 us (99%)
  between operations  0.65 us (1%)
    pallas_call x1, Pallas kernels, decode_step(): pl.pallas_call(functools.partial(step_kernel, n_tp), out_shape=tuple((plt...  57.4 us
    pallas_call x1, Pallas kernels, decode_step(): pl.pallas_call(write_kernel, out_shape=tuple((jax.ShapeDtypeStruct(o.shap...  4.14 us

profile of v2, /device:TPU:81, one launch (start us, length us, event | category | flops | bytes accessed | tf_op | source)
XLA Modules:
  0.0 62.2 jit_solution(15574380471391412773)
XLA Ops:
  0.6 57.4 %decode_step.1 = (bf16[2,3840]{1,0:T(2,128)(2,1)S(1)}, bf16[2,1024,256]{2,1,0:T(8,128)(2,1)S(1)}, bf16[2,1024,256]{2,1,0:T(8,128)(2,1)S(1)}, bf16[2,4096,256]{2,1,0:T(8,128)(2,1)S(1)}, bf16[2,4096,256]{2,1,0:T(8,128)(2,1)S(1)}) custom-call(s32[2]{0:T(128)} %pos_in.1, bf16[2,3840]{1,0:T(2,128)(2,1)} %hid_in.1, f32[1,128]{1,0:T(1,128)} %constant.9.freq_in, ...), custom_call_target="tpu_custom_call" | custom-call | tf_op jit(solution)/shard_map/decode_step/pallas_call | solution.py:335
  58.1 4.1 %write_out.1 = (bf16[2,3840]{1,0:T(2,128)(2,1)}, bf16[2,1024,256]{2,1,0:T(8,128)(2,1)}, bf16[2,1024,256]{2,1,0:T(8,128)(2,1)}, bf16[2,4096,256]{2,1,0:T(8,128)(2,1)}, bf16[2,4096,256]{2,1,0:T(8,128)(2,1)}) custom-call(bf16[2,3840]{1,0:T(2,128)(2,1)S(1)} %get-tuple-element.15.refs_0_, bf16[2,1024,256]{2,1,0:T(8,128)(2,1)S(1)} %get-tuple-element.16.refs_1_, ...), custom_call_target="tpu_custom_call" | custom-call | tf_op jit(solution)/shard_map/write_out/pallas_call | solution.py:367

commit v3 on v2

--- a/solution.py
+++ b/solution.py
@@ -18,6 +18,8 @@
 KV_STEP = 1024
 GU_GROUP = 5
 DN_GROUP = 3
+QKV_CHUNKS, CACHE_CHUNKS = 4, 3
+START_WINDOW, WINDOW, SUM_WINDOW = 10, 8, 14
 
 VMEM_LIMIT = 52 * 1024 * 1024
 
@@ -26,8 +28,8 @@
 MESH = pl.DeviceIdType.MESH
 
 
-def rem(a, b):
-    return a % b if isinstance(a, int) else lax.rem(a, b)
+def split(count, group):
+    return [min(group, count - i) for i in range(0, count, group)]
 
 
 def rms_norm(values, gain_row):
@@ -50,7 +52,6 @@
     dn_rest = ff - n_dn * CHUNK
     at_gu, at_dn = n_wo, n_wo + n_gu
     per_layer = n_wo + n_gu + n_dn + (1 if dn_rest else 0)
-    n_chunks = layers * per_layer
     me = lax.axis_index('tp')
 
     def chunk_copies(kind, layer, k, slot):
@@ -65,71 +66,64 @@
             return [pltpu.make_async_copy(wd.at[layer, pl.ds(k * CHUNK, CHUNK)], ring.at[slot], ring_sem.at[slot, 0])]
         return [pltpu.make_async_copy(wd.at[layer, pl.ds(n_dn * CHUNK, dn_rest)], ring.at[slot, pl.ds(0, dn_rest)], ring_sem.at[slot, 0])]
 
-    def start_chunk(c):
-        slot = rem(c, SLOTS)
-        layer = c // per_layer
-        r = c - layer * per_layer
-
-        def go(kind, k):
-            for copy in chunk_copies(kind, layer, k, slot):
-                copy.start()
-
-        if isinstance(c, int):
-            if c >= n_chunks:
+    def chunk_of(c):
+        layer, r = divmod(c, per_layer)
+        if r < at_gu:
+            return 'wo', layer, r
+        if r < at_dn:
+            return 'gu', layer, r - at_gu
+        if r < at_dn + n_dn:
+            return 'dn', layer, r - at_dn
+        return 'rest', layer, 0
+
+    queue = []
+    for layer in range(layers):
+        queue += [('qkv', layer), ('cache', layer)]
+        queue += [('chunk', c) for c in range(layer * per_layer, (layer + 1) * per_layer)]
+    state = {'next': 0, 'under_way': 0, 'free_chunks': SLOTS, 'free_qkv': 1}
+    size_of = {'qkv': QKV_CHUNKS, 'cache': CACHE_CHUNKS, 'chunk': 1}
+
+    def fill(limit):
+        while state['next'] < len(queue):
+            kind, index = queue[state['next']]
+            if state['under_way'] and state['under_way'] + size_of[kind] > limit:
                 return
-            if r < at_gu:
-                go('wo', r)
-            elif r < at_dn:
-                go('gu', r - at_gu)
-            elif r < at_dn + n_dn:
-                go('dn', r - at_dn)
+            if kind == 'qkv':
+                if index >= state['free_qkv']:
+                    return
+                for j in range(QKV_PARTS):
+                    for copy in qkv_copies(index, j):
+                        copy.start()
+            elif kind == 'cache':
+                for copy in cache_copies(index):
+                    copy.start()
             else:
-                go('rest', 0)
-            return
-        live = c < n_chunks
-        pl.when(live & (r < at_gu))(lambda: go('wo', r))
-        pl.when(live & (r >= at_gu) & (r < at_dn))(lambda: go('gu', r - at_gu))
-        pl.when(live & (r >= at_dn) & (r < at_dn + n_dn))(lambda: go('dn', r - at_dn))
-        if dn_rest:
-            pl.when(live & (r == at_dn + n_dn))(lambda: go('rest', 0))
-
-    def group_dot(kind, layer, lhs_ref, first, k0, group, rest=False):
-        base = layer * per_layer + first + k0
-        slots = [rem(base + j, SLOTS) for j in range(group)]
-        for j, slot in enumerate(slots):
-            for copy in chunk_copies(kind, layer, k0 + j, slot):
-                copy.wait()
-        out = acc[...]
-        if rest:
-            rest_slot = rem(base + group, SLOTS)
-            for copy in chunk_copies('rest', layer, 0, rest_slot):
-                copy.wait()
-        for j, slot in enumerate(slots):
-            at = (k0 + j) * CHUNK
-            lhs = lhs_ref[:, pl.ds(at if isinstance(at, int) else pl.multiple_of(at, CHUNK), CHUNK)]
-            out = out + jnp.dot(lhs, ring[slot], preferred_element_type=F32)
-        if rest:
-            out = out + jnp.dot(lhs_ref[:, pl.ds(n_dn * CHUNK, dn_rest)], ring[rest_slot, pl.ds(0, dn_rest)], preferred_element_type=F32)
+                if index >= state['free_chunks']:
+                    return
+                for copy in chunk_copies(*chunk_of(index), index % SLOTS):
+                    copy.start()
+            state['under_way'] += size_of[kind]
+            state['next'] += 1
+
+    def stream_dot(lhs_ref, layer, first, groups):
+        out = jnp.zeros(acc.shape, F32)
+        row = 0
+        c = layer * per_layer + first
+        for group in groups:
+            members = range(c, c + group)
+            for i in members:
+                for copy in chunk_copies(*chunk_of(i), i % SLOTS):
+                    copy.wait()
+            state['under_way'] -= group
+            fill(WINDOW)
+            for i in members:
+                n = dn_rest if chunk_of(i)[0] == 'rest' else CHUNK
+                out = out + jnp.dot(lhs_ref[:, pl.ds(row, n)], ring[i % SLOTS, pl.ds(0, n)], preferred_element_type=F32)
+                row += n
+            state['free_chunks'] += group
+            c += group
         acc[...] = out
-        for j in range(group + (1 if rest else 0)):
-            start_chunk(base + j + SLOTS)
-
-    def stream_dot(kind, layer, lhs_ref, first, count, group, rest=False):
-        acc[...] = jnp.zeros_like(acc)
-        steps, left = divmod(count, group)
-        if rest and not left:
-            steps, left = steps - 1, group
-
-        def body(i, carry):
-            group_dot(kind, layer, lhs_ref, first, i * group, group)
-            return carry
-
-        if steps == 1:
-            body(0, 0)
-        else:
-            lax.fori_loop(0, steps, body, 0)
-        if left or rest:
-            group_dot(kind, layer, lhs_ref, first, steps * group, left, rest)
+        fill(WINDOW)
 
     qkv_rows = width // QKV_PARTS
 
@@ -158,6 +152,7 @@
         copies = send_copies(phase)
         for copy in copies:
             copy.start()
+        fill(SUM_WINDOW)
         if meanwhile is not None:
             meanwhile()
         for copy in copies:
@@ -211,16 +206,17 @@
             q = q + jnp.dot(lhs, bq[piece], preferred_element_type=F32)
             k = k + jnp.dot(lhs, bk[piece], preferred_element_type=F32)
             v = v + jnp.dot(lhs, bv[piece], preferred_element_type=F32)
-        if layer + 1 < layers:
-            for j in range(QKV_PARTS):
-                for copy in qkv_copies(layer + 1, j):
-                    copy.start()
+        state['under_way'] -= QKV_CHUNKS
+        state['free_qkv'] += 1
+        fill(WINDOW)
         group = hq // head
         queries = jnp.concatenate([rotate(q[:, g * head:(g + 1) * head], trig) for g in range(group)], axis=0).astype(BF16)
         k_new = rotate(k, trig).astype(BF16)
         v_new = v.astype(BF16)
         for copy in cache_copies(layer):
             copy.wait()
+        state['under_way'] -= CACHE_CHUNKS
+        fill(WINDOW)
         q_rows = group * rows
         row_seq = lax.rem(lax.broadcasted_iota(jnp.int32, (q_rows, 1), 0), rows)
         last, slot = jnp.zeros((q_rows, 1), jnp.int32), jnp.zeros((q_rows, 1), jnp.int32)
@@ -271,15 +267,7 @@
         ((hid_in, hid_ref), (norm_in, norm_ref), (pos_in, pos_ref), (freq_in, freq_ref)))]
     for copy in small:
         copy.start()
-    for j in range(QKV_PARTS):
-        for copy in qkv_copies(0, j):
-            copy.start()
-    for copy in cache_copies(0):
-        copy.start()
-    for c in range(min(SLOTS, n_chunks)):
-        start_chunk(c)
-    for copy in cache_copies(1):
-        copy.start()
+    fill(START_WINDOW)
 
     barrier = pltpu.get_barrier_semaphore()
     for step in range(1, n_tp):
@@ -297,15 +285,15 @@
     for layer in range(layers):
         kc, vc = (kl, vl) if layer == 0 else (kg, vg)
         store_new = attention(layer, kc, vc, trig)
-        stream_dot('wo', layer, o_ref, 0, n_wo, n_wo)
+        stream_dot(o_ref, layer, 0, (n_wo,))
         if layer == 0:
             pl.semaphore_wait(barrier, n_tp - 1)
         x = add_normed(layer, 1, exchange(2 * layer, store_new))
         a_ref[...] = rms_norm(x.astype(F32), gain(layer, 2))
-        stream_dot('gu', layer, a_ref, at_gu, n_gu, GU_GROUP)
+        stream_dot(a_ref, layer, at_gu, split(n_gu, GU_GROUP))
         gate_up = acc[...]
         h_ref[...] = (jax.nn.gelu(gate_up[:, :ff], approximate=True) * gate_up[:, ff:]).astype(BF16)
-        stream_dot('dn', layer, h_ref, at_dn, n_dn, DN_GROUP, dn_rest > 0)
+        stream_dot(h_ref, layer, at_dn, split(per_layer - at_dn, DN_GROUP))
         x = add_normed(layer, 3, exchange(2 * layer + 1))
     hid_out[...] = x
     for phase in range(2 * layers):

time: 62.3 us -> 56.1 us (0.900)
  Pallas kernels: 61.6 us -> 55.2 us
    pallas_call x1, Pallas kernels: 57.4 us -> 51.1 us  [decode_step(): pl.pallas_call(functools.partial(step_kernel, n_tp), out_shape=tuple((plt...]
where the time goes in v3:
time: 56.1 us; the launch traced here: 56 us
  Pallas kernels  55.2 us (98%)
  between operations  0.81 us (1%)
    pallas_call x1, Pallas kernels, decode_step(): pl.pallas_call(functools.partial(step_kernel, n_tp), out_shape=tuple((plt...  51.1 us
    pallas_call x1, Pallas kernels, decode_step(): pl.pallas_call(write_kernel, out_shape=tuple((jax.ShapeDtypeStruct(o.shap...  4.14 us

profile of v3, /device:TPU:81, one launch (start us, length us, event | category | flops | bytes accessed | tf_op | source)
XLA Modules:
  0.0 56.0 jit_solution(7287400521571989609)
XLA Ops:
  0.6 51.1 %decode_step.1 = (bf16[2,3840]{1,0:T(2,128)(2,1)S(1)}, bf16[2,1024,256]{2,1,0:T(8,128)(2,1)S(1)}, bf16[2,1024,256]{2,1,0:T(8,128)(2,1)S(1)}, bf16[2,4096,256]{2,1,0:T(8,128)(2,1)S(1)}, bf16[2,4096,256]{2,1,0:T(8,128)(2,1)S(1)}) custom-call(s32[2]{0:T(128)} %pos_in.1, bf16[2,3840]{1,0:T(2,128)(2,1)} %hid_in.1, f32[1,128]{1,0:T(1,128)} %constant.9.freq_in, ...), custom_call_target="tpu_custom_call" | custom-call | tf_op jit(solution)/shard_map/decode_step/pallas_call | solution.py:323
  51.7 4.1 %write_out.1 = (bf16[2,3840]{1,0:T(2,128)(2,1)}, bf16[2,1024,256]{2,1,0:T(8,128)(2,1)}, bf16[2,1024,256]{2,1,0:T(8,128)(2,1)}, bf16[2,4096,256]{2,1,0:T(8,128)(2,1)}, bf16[2,4096,256]{2,1,0:T(8,128)(2,1)}) custom-call(bf16[2,3840]{1,0:T(2,128)(2,1)S(1)} %get-tuple-element.15.refs_0_, bf16[2,1024,256]{2,1,0:T(8,128)(2,1)S(1)} %get-tuple-element.16.refs_1_, ...), custom_call_target="tpu_custom_call" | custom-call | tf_op jit(solution)/shard_map/write_out/pallas_call | solution.py:355

commit v4 on v3

--- a/solution.py
+++ b/solution.py
@@ -15,17 +15,21 @@
 CHUNK = 256
 SLOTS = 22
 QKV_PARTS = 5
-KV_STEP = 1024
+KV_STEP = 2048
 GU_GROUP = 5
 DN_GROUP = 3
 QKV_CHUNKS, CACHE_CHUNKS = 4, 3
-START_WINDOW, WINDOW, SUM_WINDOW = 10, 8, 14
+START_WINDOW, WINDOW, SUM_WINDOW = 10, 8, 20
 
 VMEM_LIMIT = 52 * 1024 * 1024
 
 F32 = jnp.float32
 BF16 = jnp.bfloat16
 MESH = pl.DeviceIdType.MESH
+
+
+def rem(a, b):
+    return a % b if isinstance(a, int) else lax.rem(a, b)
 
 
 def split(count, group):
@@ -83,8 +87,11 @@
     state = {'next': 0, 'under_way': 0, 'free_chunks': SLOTS, 'free_qkv': 1}
     size_of = {'qkv': QKV_CHUNKS, 'cache': CACHE_CHUNKS, 'chunk': 1}
 
-    def fill(limit):
-        while state['next'] < len(queue):
+    def started(*item):
+        assert queue.index(item) < state['next'], item
+
+    def fill(limit, stop=None):
+        while state['next'] < len(queue) and queue[state['next']] != stop:
             kind, index = queue[state['next']]
             if state['under_way'] and state['under_way'] + size_of[kind] > limit:
                 return
@@ -112,6 +119,7 @@
         for group in groups:
             members = range(c, c + group)
             for i in members:
+                started('chunk', i)
                 for copy in chunk_copies(*chunk_of(i), i % SLOTS):
                     copy.wait()
             state['under_way'] -= group
@@ -125,6 +133,39 @@
         acc[...] = out
         fill(WINDOW)
 
+    def stream_loop(lhs_ref, layer, first, kind, steps, group, in_loop):
+        base = layer * per_layer + first
+        acc[...] = jnp.zeros_like(acc)
+        ahead = 0
+        if state['next'] < len(queue) and queue[state['next']] == ('chunk', base + steps * group):
+            ahead = min(in_loop, n_dn // steps)
+        for _ in range(ahead * steps):
+            assert chunk_of(queue[state['next']][1])[0] == 'dn' and queue[state['next']][1] < base + SLOTS
+            state['next'] += 1
+            state['under_way'] += 1
+
+        started('chunk', base + steps * group - 1)
+
+        def body(i, carry):
+            members = [(i * group + j, rem(base + i * group + j, SLOTS)) for j in range(group)]
+            for k, slot in members:
+                for copy in chunk_copies(kind, layer, k, slot):
+                    copy.wait()
+            for j in range(ahead):
+                for copy in chunk_copies('dn', layer, i * ahead + j, rem(base + steps * group + i * ahead + j, SLOTS)):
+                    copy.start()
+            out = acc[...]
+            for k, slot in members:
+                lhs = lhs_ref[:, pl.ds(pl.multiple_of(k * CHUNK, CHUNK), CHUNK)]
+                out = out + jnp.dot(lhs, ring[slot], preferred_element_type=F32)
+            acc[...] = out
+            return carry
+
+        lax.fori_loop(0, steps, body, 0)
+        state['under_way'] -= steps * group
+        state['free_chunks'] += steps * group
+        fill(WINDOW)
+
     qkv_rows = width // QKV_PARTS
 
     def qkv_copies(layer, j):
@@ -147,12 +188,12 @@
                 device_id={'tp': peer}, device_id_type=MESH))
         return copies
 
-    def exchange(phase, meanwhile=None):
+    def exchange(phase, limit, stop=None, meanwhile=None):
         part[phase, me] = acc[...].astype(BF16)
         copies = send_copies(phase)
         for copy in copies:
             copy.start()
-        fill(SUM_WINDOW)
+        fill(limit, stop)
         if meanwhile is not None:
             meanwhile()
         for copy in copies:
@@ -192,20 +233,21 @@
         a_ref[...] = rms_norm(x_ref[...], gain(layer, 0))
         hq = bq.shape[1]
 
-        q, k, v = jnp.zeros((rows, hq), F32), jnp.zeros((rows, head), F32), jnp.zeros((rows, head), F32)
-        if layer > 0:
-            for j in range(QKV_PARTS):
-                for copy in qkv_copies(layer, j):
-                    copy.wait()
-        for j in range(QKV_PARTS):
-            if layer == 0:
-                for copy in qkv_copies(layer, j):
-                    copy.wait()
-            piece = pl.ds(j * qkv_rows, qkv_rows)
+        started('qkv', layer)
+
+        def qkv_body(j, carry):
+            q, k, v = carry
+            for copy in qkv_copies(layer, j):
+                copy.wait()
+            piece = pl.ds(pl.multiple_of(j * qkv_rows, qkv_rows), qkv_rows)
             lhs = a_ref[:, piece]
             q = q + jnp.dot(lhs, bq[piece], preferred_element_type=F32)
             k = k + jnp.dot(lhs, bk[piece], preferred_element_type=F32)
             v = v + jnp.dot(lhs, bv[piece], preferred_element_type=F32)
+            return q, k, v
+
+        q, k, v = lax.fori_loop(0, QKV_PARTS, qkv_body, (
+            jnp.zeros((rows, hq), F32), jnp.zeros((rows, head), F32), jnp.zeros((rows, head), F32)))
         state['under_way'] -= QKV_CHUNKS
         state['free_qkv'] += 1
         fill(WINDOW)
@@ -213,6 +255,7 @@
         queries = jnp.concatenate([rotate(q[:, g * head:(g + 1) * head], trig) for g in range(group)], axis=0).astype(BF16)
         k_new = rotate(k, trig).astype(BF16)
         v_new = v.astype(BF16)
+        started('cache', layer)
         for copy in cache_copies(layer):
             copy.wait()
         state['under_way'] -= CACHE_CHUNKS
@@ -239,19 +282,23 @@
         per_row = [jnp.concatenate([new.astype(F32)] * group, axis=0) for new in (k_new, v_new)]
         e_new = soft_exp(jnp.sum(queries.astype(F32) * per_row[0], axis=-1, keepdims=True))
         total = e_new
-        weights = []
-        for i in range(n // step):
-            piece = pl.ds(i * step, step)
+        def score_body(i, total):
+            piece = pl.ds(pl.multiple_of(i * step, step), step)
             s = pick([lax.dot_general(queries, kc[b, piece], contract_last, preferred_element_type=F32) for b in range(rows)])
             ids = lax.broadcasted_iota(jnp.int32, (q_rows, step), 1) + i * step
             e = jnp.where((ids <= last) & (ids != slot), soft_exp(s), 0.0)
             e_ref[:, piece] = e
-            total = total + jnp.sum(e, axis=-1, keepdims=True)
+            return total + jnp.sum(e, axis=-1, keepdims=True)
+
+        total = lax.fori_loop(0, n // step, score_body, total)
+
+        def value_body(i, out):
+            piece = pl.ds(pl.multiple_of(i * step, step), step)
+            probs = (e_ref[:, piece] / total).astype(BF16)
+            return out + pick([jnp.dot(probs, vc[b, piece], preferred_element_type=F32) for b in range(rows)])
+
         out = (e_new / total).astype(BF16).astype(F32) * per_row[1]
-        for i in range(n // step):
-            piece = pl.ds(i * step, step)
-            probs = (e_ref[:, piece] / total).astype(BF16)
-            out = out + pick([jnp.dot(probs, vc[b, piece], preferred_element_type=F32) for b in range(rows)])
+        out = lax.fori_loop(0, n // step, value_body, out)
         mixed = out.astype(BF16)
         for g in range(group):
             o_ref[:, pl.ds(g * head, head)] = mixed[g * rows:(g + 1) * rows]
@@ -288,13 +335,13 @@
         stream_dot(o_ref, layer, 0, (n_wo,))
         if layer == 0:
             pl.semaphore_wait(barrier, n_tp - 1)
-        x = add_normed(layer, 1, exchange(2 * layer, store_new))
+        x = add_normed(layer, 1, exchange(2 * layer, len(queue) * QKV_CHUNKS, ('chunk', at_dn), store_new))
         a_ref[...] = rms_norm(x.astype(F32), gain(layer, 2))
-        stream_dot(a_ref, layer, at_gu, split(n_gu, GU_GROUP))
+        stream_loop(a_ref, layer, at_gu, 'gu', n_gu // GU_GROUP, GU_GROUP, 2)
         gate_up = acc[...]
         h_ref[...] = (jax.nn.gelu(gate_up[:, :ff], approximate=True) * gate_up[:, ff:]).astype(BF16)
         stream_dot(h_ref, layer, at_dn, split(per_layer - at_dn, DN_GROUP))
-        x = add_normed(layer, 3, exchange(2 * layer + 1))
+        x = add_normed(layer, 3, exchange(2 * layer + 1, SUM_WINDOW))
     hid_out[...] = x
     for phase in range(2 * layers):
         for copy in send_copies(phase):

time: 56.1 us -> 52.3 us (0.932)
  Pallas kernels: 55.2 us -> 51.6 us
    pallas_call x1, Pallas kernels: 51.1 us -> 47.4 us  [decode_step(): pl.pallas_call(functools.partial(step_kernel, n_tp), out_shape=tuple((plt...]
where the time goes in v4:
time: 52.3 us; the launch traced here: 52.2 us
  Pallas kernels  51.6 us (99%)
  between operations  0.65 us (1%)
    pallas_call x1, Pallas kernels, decode_step(): pl.pallas_call(functools.partial(step_kernel, n_tp), out_shape=tuple((plt...  47.4 us
    pallas_call x1, Pallas kernels, decode_step(): pl.pallas_call(write_kernel, out_shape=tuple((jax.ShapeDtypeStruct(o.shap...  4.14 us

profile of v4, /device:TPU:81, one launch (start us, length us, event | category | flops | bytes accessed | tf_op | source)
XLA Modules:
  0.0 52.2 jit_solution(5798552087731683886)
XLA Ops:
  0.6 47.4 %decode_step.1 = (bf16[2,3840]{1,0:T(2,128)(2,1)S(1)}, bf16[2,1024,256]{2,1,0:T(8,128)(2,1)S(1)}, bf16[2,1024,256]{2,1,0:T(8,128)(2,1)S(1)}, bf16[2,4096,256]{2,1,0:T(8,128)(2,1)S(1)}, bf16[2,4096,256]{2,1,0:T(8,128)(2,1)S(1)}) custom-call(s32[2]{0:T(128)} %pos_in.1, bf16[2,3840]{1,0:T(2,128)(2,1)} %hid_in.1, f32[1,128]{1,0:T(1,128)} %constant.9.freq_in, ...), custom_call_target="tpu_custom_call" | custom-call | tf_op jit(solution)/shard_map/decode_step/pallas_call | solution.py:370
  48.1 4.1 %write_out.1 = (bf16[2,3840]{1,0:T(2,128)(2,1)}, bf16[2,1024,256]{2,1,0:T(8,128)(2,1)}, bf16[2,1024,256]{2,1,0:T(8,128)(2,1)}, bf16[2,4096,256]{2,1,0:T(8,128)(2,1)}, bf16[2,4096,256]{2,1,0:T(8,128)(2,1)}) custom-call(bf16[2,3840]{1,0:T(2,128)(2,1)S(1)} %get-tuple-element.15.refs_0_, bf16[2,1024,256]{2,1,0:T(8,128)(2,1)S(1)} %get-tuple-element.16.refs_1_, ...), custom_call_target="tpu_custom_call" | custom-call | tf_op jit(solution)/shard_map/write_out/pallas_call | solution.py:402

commit v5 on v4

--- a/solution.py
+++ b/solution.py
@@ -14,7 +14,7 @@
 
 CHUNK = 256
 SLOTS = 22
-QKV_PARTS = 5
+QKV_PARTS = 3
 KV_STEP = 2048
 GU_GROUP = 5
 DN_GROUP = 3
@@ -57,6 +57,8 @@
     at_gu, at_dn = n_wo, n_wo + n_gu
     per_layer = n_wo + n_gu + n_dn + (1 if dn_rest else 0)
     me = lax.axis_index('tp')
+    cut = pl.cdiv(width, 2 * CHUNK) * CHUNK
+    pieces = ((0, cut), (cut, width - cut))
 
     def chunk_copies(kind, layer, k, slot):
         if kind == 'wo':
@@ -112,11 +114,11 @@
             state['under_way'] += size_of[kind]
             state['next'] += 1
 
-    def stream_dot(lhs_ref, layer, first, groups):
-        out = jnp.zeros(acc.shape, F32)
+    def stream_dot(lhs_ref, layer, first, groups, phase):
+        out = None
         row = 0
         c = layer * per_layer + first
-        for group in groups:
+        for g, group in enumerate(groups):
             members = range(c, c + group)
             for i in members:
                 started('chunk', i)
@@ -124,14 +126,28 @@
                     copy.wait()
             state['under_way'] -= group
             fill(WINDOW)
+            terms = []
             for i in members:
                 n = dn_rest if chunk_of(i)[0] == 'rest' else CHUNK
-                out = out + jnp.dot(lhs_ref[:, pl.ds(row, n)], ring[i % SLOTS, pl.ds(0, n)], preferred_element_type=F32)
+                terms.append((lhs_ref[:, pl.ds(row, n)], i % SLOTS, n))
                 row += n
+
+            def product(columns):
+                start, size = columns
+                parts = [] if out is None else [out[:, start:start + size]]
+                for lhs, slot, n in terms:
+                    parts.append(jnp.dot(lhs, ring[slot, pl.ds(0, n), pl.ds(start, size)], preferred_element_type=F32))
+                return functools.reduce(jnp.add, parts)
+
             state['free_chunks'] += group
             c += group
-        acc[...] = out
-        fill(WINDOW)
+            if g < len(groups) - 1:
+                out = product((0, width))
+                continue
+            for p, columns in enumerate(pieces):
+                part[phase, me, :, pl.ds(*columns)] = product(columns).astype(BF16)
+                for copy in send_copies(phase, p):
+                    copy.start()
 
     def stream_loop(lhs_ref, layer, first, kind, steps, group, in_loop):
         base = layer * per_layer + first
@@ -178,30 +194,30 @@
         return [pltpu.make_async_copy(src.at[b], dst.at[b], cache_sem.at[layer, i, b])
                 for i, (src, dst) in enumerate(pairs) for b in range(rows)]
 
-    def send_copies(phase):
+    def send_copies(phase, p):
         copies = []
         for step in range(1, n_tp):
             peer = lax.rem(me + step, n_tp)
+            mine = part.at[phase, me, :, pl.ds(*pieces[p])]
             copies.append(pltpu.make_async_remote_copy(
-                src_ref=part.at[phase, me], dst_ref=part.at[phase, me],
-                send_sem=send_sem.at[phase, step - 1], recv_sem=recv_sem.at[phase, step - 1],
+                src_ref=mine, dst_ref=mine,
+                send_sem=send_sem.at[phase, p, step - 1], recv_sem=recv_sem.at[phase, p, step - 1],
                 device_id={'tp': peer}, device_id_type=MESH))
         return copies
 
-    def exchange(phase, limit, stop=None, meanwhile=None):
-        part[phase, me] = acc[...].astype(BF16)
-        copies = send_copies(phase)
-        for copy in copies:
-            copy.start()
+    def collect(phase, limit, stop=None, meanwhile=None):
         fill(limit, stop)
         if meanwhile is not None:
             meanwhile()
-        for copy in copies:
-            copy.wait_recv()
-        total = part[phase, 0].astype(F32)
-        for j in range(1, n_tp):
-            total = total + part[phase, j].astype(F32)
-        return total
+        sums = []
+        for p, columns in enumerate(pieces):
+            for copy in send_copies(phase, p):
+                copy.wait_recv()
+            total = part[phase, 0, :, pl.ds(*columns)].astype(F32)
+            for j in range(1, n_tp):
+                total = total + part[phase, j, :, pl.ds(*columns)].astype(F32)
+            sums.append(total)
+        return jnp.concatenate(sums, axis=-1)
 
     def gain(layer, i):
         return norm_ref[layer, pl.ds(i, 1), :]
@@ -277,7 +293,7 @@
         contract_last = (((1,), (1,)), ((), ()))
 
         def soft_exp(s):
-            return jnp.exp(SOFT_CAP * jnp.tanh(s * head ** -0.5 / SOFT_CAP))
+            return jnp.exp(SOFT_CAP * jnp.tanh(s * (head ** -0.5 / SOFT_CAP)))
 
         per_row = [jnp.concatenate([new.astype(F32)] * group, axis=0) for new in (k_new, v_new)]
         e_new = soft_exp(jnp.sum(queries.astype(F32) * per_row[0], axis=-1, keepdims=True))
@@ -294,10 +310,11 @@
 
         def value_body(i, out):
             piece = pl.ds(pl.multiple_of(i * step, step), step)
-            probs = (e_ref[:, piece] / total).astype(BF16)
+            probs = (e_ref[:, piece] * inv_total).astype(BF16)
             return out + pick([jnp.dot(probs, vc[b, piece], preferred_element_type=F32) for b in range(rows)])
 
-        out = (e_new / total).astype(BF16).astype(F32) * per_row[1]
+        inv_total = 1.0 / total
+        out = (e_new * inv_total).astype(BF16).astype(F32) * per_row[1]
         out = lax.fori_loop(0, n // step, value_body, out)
         mixed = out.astype(BF16)
         for g in range(group):
@@ -332,20 +349,21 @@
     for layer in range(layers):
         kc, vc = (kl, vl) if layer == 0 else (kg, vg)
         store_new = attention(layer, kc, vc, trig)
-        stream_dot(o_ref, layer, 0, (n_wo,))
         if layer == 0:
             pl.semaphore_wait(barrier, n_tp - 1)
-        x = add_normed(layer, 1, exchange(2 * layer, len(queue) * QKV_CHUNKS, ('chunk', at_dn), store_new))
+        stream_dot(o_ref, layer, 0, (n_wo,), 2 * layer)
+        x = add_normed(layer, 1, collect(2 * layer, len(queue) * QKV_CHUNKS, ('chunk', at_dn), store_new))
         a_ref[...] = rms_norm(x.astype(F32), gain(layer, 2))
         stream_loop(a_ref, layer, at_gu, 'gu', n_gu // GU_GROUP, GU_GROUP, 2)
         gate_up = acc[...]
         h_ref[...] = (jax.nn.gelu(gate_up[:, :ff], approximate=True) * gate_up[:, ff:]).astype(BF16)
-        stream_dot(h_ref, layer, at_dn, split(per_layer - at_dn, DN_GROUP))
-        x = add_normed(layer, 3, exchange(2 * layer + 1, SUM_WINDOW))
+        stream_dot(h_ref, layer, at_dn, split(per_layer - at_dn, DN_GROUP), 2 * layer + 1)
+        x = add_normed(layer, 3, collect(2 * layer + 1, SUM_WINDOW))
     hid_out[...] = x
     for phase in range(2 * layers):
-        for copy in send_copies(phase):
-            copy.wait_send()
+        for p in range(len(pieces)):
+            for copy in send_copies(phase, p):
+                copy.wait_send()
 
 
 def write_kernel(*refs):
@@ -392,8 +410,8 @@
             pltpu.SemaphoreType.DMA((SLOTS, 2)),
             pltpu.SemaphoreType.DMA((3, QKV_PARTS)),
             pltpu.SemaphoreType.DMA((2, 2, rows)),
-            pltpu.SemaphoreType.DMA((2 * layers, n_tp - 1)),
-            pltpu.SemaphoreType.DMA((2 * layers, n_tp - 1)),
+            pltpu.SemaphoreType.DMA((2 * layers, 2, n_tp - 1)),
+            pltpu.SemaphoreType.DMA((2 * layers, 2, n_tp - 1)),
         ],
         compiler_params=pltpu.CompilerParams(
             collective_id=0, has_side_effects=True, vmem_limit_bytes=VMEM_LIMIT),

time: 52.3 us -> 52.2 us (level)
  no operation moved by 1% of the time
where the time goes in v5:
time: 52.2 us
  Pallas kernels  51.4 us (98%)
  between operations  0.81 us (2%)
    pallas_call x1, Pallas kernels, decode_step(): pl.pallas_call(functools.partial(step_kernel, n_tp), out_shape=tuple((plt...  47.2 us
    pallas_call x1, Pallas kernels, decode_step(): pl.pallas_call(write_kernel, out_shape=tuple((jax.ShapeDtypeStruct(o.shap...  4.14 us

profile of v5, /device:TPU:81, one launch (start us, length us, event | category | flops | bytes accessed | tf_op | source)
XLA Modules:
  0.0 52.2 jit_solution(6203991443989246918)
XLA Ops:
  0.6 47.2 %decode_step.1 = (bf16[2,3840]{1,0:T(2,128)(2,1)S(1)}, bf16[2,1024,256]{2,1,0:T(8,128)(2,1)S(1)}, bf16[2,1024,256]{2,1,0:T(8,128)(2,1)S(1)}, bf16[2,4096,256]{2,1,0:T(8,128)(2,1)S(1)}, bf16[2,4096,256]{2,1,0:T(8,128)(2,1)S(1)}) custom-call(s32[2]{0:T(128)} %pos_in.1, bf16[2,3840]{1,0:T(2,128)(2,1)} %hid_in.1, f32[1,128]{1,0:T(1,128)} %constant.9.freq_in, ...), custom_call_target="tpu_custom_call" | custom-call | tf_op jit(solution)/shard_map/decode_step/pallas_call | solution.py:388
  47.9 4.1 %write_out.1 = (bf16[2,3840]{1,0:T(2,128)(2,1)}, bf16[2,1024,256]{2,1,0:T(8,128)(2,1)}, bf16[2,1024,256]{2,1,0:T(8,128)(2,1)}, bf16[2,4096,256]{2,1,0:T(8,128)(2,1)}, bf16[2,4096,256]{2,1,0:T(8,128)(2,1)}) custom-call(bf16[2,3840]{1,0:T(2,128)(2,1)S(1)} %get-tuple-element.15.refs_0_, bf16[2,1024,256]{2,1,0:T(8,128)(2,1)S(1)} %get-tuple-element.16.refs_1_, ...), custom_call_target="tpu_custom_call" | custom-call | tf_op jit(solution)/shard_map/write_out/pallas_call | solution.py:420

commit v6 on v4

--- a/solution.py
+++ b/solution.py
@@ -14,7 +14,7 @@
 
 CHUNK = 256
 SLOTS = 22
-QKV_PARTS = 5
+QKV_PARTS = 3
 KV_STEP = 2048
 GU_GROUP = 5
 DN_GROUP = 3
@@ -30,6 +30,10 @@
 
 def rem(a, b):
     return a % b if isinstance(a, int) else lax.rem(a, b)
+
+
+def far_first(n_tp):
+    return sorted(range(1, n_tp), key=lambda step: -min(step, n_tp - step))
 
 
 def split(count, group):
@@ -60,15 +64,19 @@
 
     def chunk_copies(kind, layer, k, slot):
         if kind == 'wo':
-            return [pltpu.make_async_copy(wo.at[layer, pl.ds(k * CHUNK, CHUNK)], ring.at[slot], ring_sem.at[slot, 0])]
+            return [pltpu.make_async_copy(wo.at[layer, pl.ds(k * CHUNK, CHUNK)], ring.at[slot], ring_sem.at[slot])]
         if kind == 'gu':
             return [
-                pltpu.make_async_copy(wg.at[layer, pl.ds(k * CHUNK, CHUNK)], ring.at[slot, :, pl.ds(0, ff)], ring_sem.at[slot, 0]),
-                pltpu.make_async_copy(wu.at[layer, pl.ds(k * CHUNK, CHUNK)], ring.at[slot, :, pl.ds(ff, ff)], ring_sem.at[slot, 1]),
+                pltpu.make_async_copy(wg.at[layer, pl.ds(k * CHUNK, CHUNK)], ring.at[slot, :, pl.ds(0, ff)], ring_sem.at[slot]),
+                pltpu.make_async_copy(wu.at[layer, pl.ds(k * CHUNK, CHUNK)], ring.at[slot, :, pl.ds(ff, ff)], ring_sem.at[slot]),
             ]
         if kind == 'dn':
-            return [pltpu.make_async_copy(wd.at[layer, pl.ds(k * CHUNK, CHUNK)], ring.at[slot], ring_sem.at[slot, 0])]
-        return [pltpu.make_async_copy(wd.at[layer, pl.ds(n_dn * CHUNK, dn_rest)], ring.at[slot, pl.ds(0, dn_rest)], ring_sem.at[slot, 0])]
+            return [pltpu.make_async_copy(wd.at[layer, pl.ds(k * CHUNK, CHUNK)], ring.at[slot], ring_sem.at[slot])]
+        return [pltpu.make_async_copy(wd.at[layer, pl.ds(n_dn * CHUNK, dn_rest)], ring.at[slot, pl.ds(0, dn_rest)], ring_sem.at[slot])]
+
+    def wait_chunk(kind, slot):
+        place = ring.at[slot, pl.ds(0, dn_rest)] if kind == 'rest' else ring.at[slot]
+        pltpu.make_async_copy(place, place, ring_sem.at[slot]).wait()
 
     def chunk_of(c):
         layer, r = divmod(c, per_layer)
@@ -120,8 +128,7 @@
             members = range(c, c + group)
             for i in members:
                 started('chunk', i)
-                for copy in chunk_copies(*chunk_of(i), i % SLOTS):
-                    copy.wait()
+                wait_chunk(chunk_of(i)[0], i % SLOTS)
             state['under_way'] -= group
             fill(WINDOW)
             for i in members:
@@ -149,8 +156,7 @@
         def body(i, carry):
             members = [(i * group + j, rem(base + i * group + j, SLOTS)) for j in range(group)]
             for k, slot in members:
-                for copy in chunk_copies(kind, layer, k, slot):
-                    copy.wait()
+                wait_chunk(kind, slot)
             for j in range(ahead):
                 for copy in chunk_copies('dn', layer, i * ahead + j, rem(base + steps * group + i * ahead + j, SLOTS)):
                     copy.start()
@@ -180,13 +186,19 @@
 
     def send_copies(phase):
         copies = []
-        for step in range(1, n_tp):
+        for step in far_first(n_tp):
             peer = lax.rem(me + step, n_tp)
             copies.append(pltpu.make_async_remote_copy(
                 src_ref=part.at[phase, me], dst_ref=part.at[phase, me],
-                send_sem=send_sem.at[phase, step - 1], recv_sem=recv_sem.at[phase, step - 1],
+                send_sem=send_sem.at[phase], recv_sem=recv_sem.at[phase],
                 device_id={'tp': peer}, device_id_type=MESH))
         return copies
+
+    def all_copies(phase):
+        blocks = part.at[phase, pl.ds(0, n_tp - 1)]
+        return pltpu.make_async_remote_copy(
+            src_ref=blocks, dst_ref=blocks, send_sem=send_sem.at[phase], recv_sem=recv_sem.at[phase],
+            device_id={'tp': me}, device_id_type=MESH)
 
     def exchange(phase, limit, stop=None, meanwhile=None):
         part[phase, me] = acc[...].astype(BF16)
@@ -196,8 +208,7 @@
         fill(limit, stop)
         if meanwhile is not None:
             meanwhile()
-        for copy in copies:
-            copy.wait_recv()
+        all_copies(phase).wait_recv()
         total = part[phase, 0].astype(F32)
         for j in range(1, n_tp):
             total = total + part[phase, j].astype(F32)
@@ -277,7 +288,7 @@
         contract_last = (((1,), (1,)), ((), ()))
 
         def soft_exp(s):
-            return jnp.exp(SOFT_CAP * jnp.tanh(s * head ** -0.5 / SOFT_CAP))
+            return jnp.exp(SOFT_CAP * jnp.tanh(s * (head ** -0.5 / SOFT_CAP)))
 
         per_row = [jnp.concatenate([new.astype(F32)] * group, axis=0) for new in (k_new, v_new)]
         e_new = soft_exp(jnp.sum(queries.astype(F32) * per_row[0], axis=-1, keepdims=True))
@@ -294,10 +305,11 @@
 
         def value_body(i, out):
             piece = pl.ds(pl.multiple_of(i * step, step), step)
-            probs = (e_ref[:, piece] / total).astype(BF16)
+            probs = (e_ref[:, piece] * inv_total).astype(BF16)
             return out + pick([jnp.dot(probs, vc[b, piece], preferred_element_type=F32) for b in range(rows)])
 
-        out = (e_new / total).astype(BF16).astype(F32) * per_row[1]
+        inv_total = 1.0 / total
+        out = (e_new * inv_total).astype(BF16).astype(F32) * per_row[1]
         out = lax.fori_loop(0, n // step, value_body, out)
         mixed = out.astype(BF16)
         for g in range(group):
@@ -344,8 +356,7 @@
         x = add_normed(layer, 3, exchange(2 * layer + 1, SUM_WINDOW))
     hid_out[...] = x
     for phase in range(2 * layers):
-        for copy in send_copies(phase):
-            copy.wait_send()
+        all_copies(phase).wait_send()
 
 
 def write_kernel(*refs):
@@ -389,11 +400,11 @@
             pltpu.VMEM((hq // head * rows, n_ctx), F32),
             pltpu.VMEM((2 * layers, n_tp, rows, width), BF16),
             pltpu.SemaphoreType.DMA((4,)),
-            pltpu.SemaphoreType.DMA((SLOTS, 2)),
+            pltpu.SemaphoreType.DMA((SLOTS,)),
             pltpu.SemaphoreType.DMA((3, QKV_PARTS)),
             pltpu.SemaphoreType.DMA((2, 2, rows)),
-            pltpu.SemaphoreType.DMA((2 * layers, n_tp - 1)),
-            pltpu.SemaphoreType.DMA((2 * layers, n_tp - 1)),
+            pltpu.SemaphoreType.DMA((2 * layers,)),
+            pltpu.SemaphoreType.DMA((2 * layers,)),
         ],
         compiler_params=pltpu.CompilerParams(
             collective_id=0, has_side_effects=True, vmem_limit_bytes=VMEM_LIMIT),

time: 52.3 us -> 50.2 us (0.960)
  Pallas kernels: 51.6 us -> 49.5 us
    pallas_call x1, Pallas kernels: 47.4 us -> 45.4 us  [decode_step(): pl.pallas_call(functools.partial(step_kernel, n_tp), out_shape=tuple((plt...]
where the time goes in v6:
time: 50.2 us; the launch traced here: 50.1 us
  Pallas kernels  49.5 us (99%)
  between operations  0.65 us (1%)
    pallas_call x1, Pallas kernels, decode_step(): pl.pallas_call(functools.partial(step_kernel, n_tp), out_shape=tuple((plt...  45.4 us
    pallas_call x1, Pallas kernels, decode_step(): pl.pallas_call(write_kernel, out_shape=tuple((jax.ShapeDtypeStruct(o.shap...  4.14 us

profile of v6, /device:TPU:81, one launch (start us, length us, event | category | flops | bytes accessed | tf_op | source)
XLA Modules:
  0.0 50.1 jit_solution(11513683253551395056)
XLA Ops:
  0.6 45.4 %decode_step.1 = (bf16[2,3840]{1,0:T(2,128)(2,1)S(1)}, bf16[2,1024,256]{2,1,0:T(8,128)(2,1)S(1)}, bf16[2,1024,256]{2,1,0:T(8,128)(2,1)S(1)}, bf16[2,4096,256]{2,1,0:T(8,128)(2,1)S(1)}, bf16[2,4096,256]{2,1,0:T(8,128)(2,1)S(1)}) custom-call(s32[2]{0:T(128)} %pos_in.1, bf16[2,3840]{1,0:T(2,128)(2,1)} %hid_in.1, f32[1,128]{1,0:T(1,128)} %constant.9.freq_in, ...), custom_call_target="tpu_custom_call" | custom-call | tf_op jit(solution)/shard_map/decode_step/pallas_call | solution.py:381
  46.0 4.1 %write_out.1 = (bf16[2,3840]{1,0:T(2,128)(2,1)}, bf16[2,1024,256]{2,1,0:T(8,128)(2,1)}, bf16[2,1024,256]{2,1,0:T(8,128)(2,1)}, bf16[2,4096,256]{2,1,0:T(8,128)(2,1)}, bf16[2,4096,256]{2,1,0:T(8,128)(2,1)}) custom-call(bf16[2,3840]{1,0:T(2,128)(2,1)S(1)} %get-tuple-element.15.refs_0_, bf16[2,1024,256]{2,1,0:T(8,128)(2,1)S(1)} %get-tuple-element.16.refs_1_, ...), custom_call_target="tpu_custom_call" | custom-call | tf_op jit(solution)/shard_map/write_out/pallas_call | solution.py:413

commit v7 on v6

--- a/solution.py
+++ b/solution.py
@@ -18,8 +18,9 @@
 KV_STEP = 2048
 GU_GROUP = 5
 DN_GROUP = 3
+LATE_DN_GROUP = 3
 QKV_CHUNKS, CACHE_CHUNKS = 4, 3
-START_WINDOW, WINDOW, SUM_WINDOW = 10, 8, 20
+START_WINDOW, WINDOW, SUM_WINDOW = 10, 8, 32
 
 VMEM_LIMIT = 52 * 1024 * 1024
 
@@ -181,8 +182,7 @@
 
     def cache_copies(layer):
         pairs = ((kl_in, kl), (vl_in, vl)) if layer == 0 else ((kg_in, kg), (vg_in, vg))
-        return [pltpu.make_async_copy(src.at[b], dst.at[b], cache_sem.at[layer, i, b])
-                for i, (src, dst) in enumerate(pairs) for b in range(rows)]
+        return [pltpu.make_async_copy(src, dst, cache_sem.at[layer, i]) for i, (src, dst) in enumerate(pairs)]
 
     def send_copies(phase):
         copies = []
@@ -352,7 +352,7 @@
         stream_loop(a_ref, layer, at_gu, 'gu', n_gu // GU_GROUP, GU_GROUP, 2)
         gate_up = acc[...]
         h_ref[...] = (jax.nn.gelu(gate_up[:, :ff], approximate=True) * gate_up[:, ff:]).astype(BF16)
-        stream_dot(h_ref, layer, at_dn, split(per_layer - at_dn, DN_GROUP))
+        stream_dot(h_ref, layer, at_dn, split(per_layer - at_dn, DN_GROUP if layer == 0 else LATE_DN_GROUP))
         x = add_normed(layer, 3, exchange(2 * layer + 1, SUM_WINDOW))
     hid_out[...] = x
     for phase in range(2 * layers):
@@ -361,11 +361,13 @@
 
 def write_kernel(*refs):
     n = len(refs) // 2
-    copies = [pltpu.make_async_copy(refs[i], refs[n + i], refs[-1].at[i]) for i in range(n)]
-    for copy in copies:
-        copy.start()
-    for copy in copies:
-        copy.wait()
+    for i in range(n):
+        for b in range(refs[i].shape[0] if len(refs[i].shape) > 2 else 1):
+            part = refs[i].at[b] if len(refs[i].shape) > 2 else refs[i]
+            place = refs[n + i].at[b] if len(refs[i].shape) > 2 else refs[n + i]
+            pltpu.make_async_copy(part, place, refs[-1].at[i]).start()
+    for i in range(n):
+        pltpu.make_async_copy(refs[i], refs[n + i], refs[-1].at[i]).wait()
 
 
 def decode_step(n_tp, hidden, positions, k_local, v_local, k_global, v_global, w_query, w_key, w_value, w_out, w_gate, w_up, w_down, norm_scale):
@@ -402,7 +404,7 @@
             pltpu.SemaphoreType.DMA((4,)),
             pltpu.SemaphoreType.DMA((SLOTS,)),
             pltpu.SemaphoreType.DMA((3, QKV_PARTS)),
-            pltpu.SemaphoreType.DMA((2, 2, rows)),
+            pltpu.SemaphoreType.DMA((2, 2)),
             pltpu.SemaphoreType.DMA((2 * layers,)),
             pltpu.SemaphoreType.DMA((2 * layers,)),
         ],

time: 50.2 us -> 50 us (level)
  no operation moved by 1% of the time
where the time goes in v7:
time: 50 us; the launch traced here: 49.9 us
  Pallas kernels  49.2 us (98%)
  between operations  0.65 us (1%)
    pallas_call x1, Pallas kernels, decode_step(): pl.pallas_call(functools.partial(step_kernel, n_tp), out_shape=tuple((plt...  45.2 us
    pallas_call x1, Pallas kernels, decode_step(): pl.pallas_call(write_kernel, out_shape=tuple((jax.ShapeDtypeStruct(o.shap...  4.01 us

profile of v7, /device:TPU:81, one launch (start us, length us, event | category | flops | bytes accessed | tf_op | source)
XLA Modules:
  0.0 49.9 jit_solution(17753588990004332519)
XLA Ops:
  0.6 45.2 %decode_step.1 = (bf16[2,3840]{1,0:T(2,128)(2,1)S(1)}, bf16[2,1024,256]{2,1,0:T(8,128)(2,1)S(1)}, bf16[2,1024,256]{2,1,0:T(8,128)(2,1)S(1)}, bf16[2,4096,256]{2,1,0:T(8,128)(2,1)S(1)}, bf16[2,4096,256]{2,1,0:T(8,128)(2,1)S(1)}) custom-call(s32[2]{0:T(128)} %pos_in.1, bf16[2,3840]{1,0:T(2,128)(2,1)} %hid_in.1, f32[1,128]{1,0:T(1,128)} %constant.9.freq_in, ...), custom_call_target="tpu_custom_call" | custom-call | tf_op jit(solution)/shard_map/decode_step/pallas_call | solution.py:383
  45.9 4.0 %write_out.1 = (bf16[2,3840]{1,0:T(2,128)(2,1)}, bf16[2,1024,256]{2,1,0:T(8,128)(2,1)}, bf16[2,1024,256]{2,1,0:T(8,128)(2,1)}, bf16[2,4096,256]{2,1,0:T(8,128)(2,1)}, bf16[2,4096,256]{2,1,0:T(8,128)(2,1)}) custom-call(bf16[2,3840]{1,0:T(2,128)(2,1)S(1)} %get-tuple-element.15.refs_0_, bf16[2,1024,256]{2,1,0:T(8,128)(2,1)S(1)} %get-tuple-element.16.refs_1_, ...), custom_call_target="tpu_custom_call" | custom-call | tf_op jit(solution)/shard_map/write_out/pallas_call | solution.py:415
